TPU v7x, 32 devices: a whole 2x2x4 slice. The times are simulated.
32 devices in a mesh: parts: 2 (over x), rows: 16 (over z, y, core).
Axes of the slice: x: 2, y: 2, z: 4, core: 2. Of those that a mesh axis runs over, the one named last changes fastest.
Arguments:
- features: bfloat16 [128, 256, 512], P(('parts', 'rows')), parts along dimension 0, may hold values from -10 to 10, as said below
- grad_out: bfloat16 [128, 256, 512], P(('parts', 'rows')), parts along dimension 0, may hold values from -11 to 11, as said below
- filters: bfloat16 [512, 3, 3, 512], replicated, may hold values from -0.09375 to 0.09375
- norm_gain: float32 [512], replicated, may hold values from 0.25 to 1.75
- norm_bias: float32 [512], replicated, may hold values from -1 to 1
Outputs:
- grad_in: bfloat16 [128, 256, 512], P(('parts', 'rows')), parts along dimension 0
- filter_grad: float32 [1024, 3, 3, 512], P(('parts', 'rows')), parts along dimension 0
- gain_grad: float32 [1024], P('parts'), parts along dimension 0
- bias_grad: float32 [1024], P('parts'), parts along dimension 0
There are 2 independent parts, one for each index of `parts`. A program takes and returns all parts, laid end to end along the dimension named above; an argument that names none is the same for every part. Nothing has to cross between parts.
Inputs may be any that keep to these rules, and one draw needn't show every extreme that they name: `features`: each image row has its own offset and spread for each group. `grad_out`: each image row and channel has its own offset.
All inputs are finite; a program needn't handle non-finite values.
Results may differ from a plain program's by a relative error of at most 0.0005.
Values may be sent and summed in bfloat16 or wider, within the bound.
A program may use at most 128 MiB of HBM per device.

v0:
```python
import functools
import math

import jax
import jax.numpy as jnp
from jax import lax
from jax.experimental import pallas as pl
from jax.experimental.pallas import tpu as pltpu
from jax.sharding import PartitionSpec as P

GROUPS = 32
LANES = 128
POWER = 9
SPLIT = 2
LAG3 = 4
LAG4 = 8
MAIN = 60
EPSILON = 1e-06
GAIN_MAX = 1.75
BIAS_MAX = 1.0
MESH = pl.DeviceIdType.MESH
F32 = jnp.float32
BF16 = jnp.bfloat16


def encode(value):
    square = value * value
    fourth = square * square
    return (fourth * fourth * value).astype(BF16)


def decode(coded):
    wide = coded.astype(F32)
    root = jnp.exp2(jnp.log2(jnp.maximum(jnp.abs(wide), 1e-38)) * (1.0 / POWER))
    root = jnp.where(jnp.abs(wide) < 1e-37, 0.0, root)
    return jnp.where(wide < 0.0, -root, root)


def group_sum(row, per_group):
    value = jnp.broadcast_to(row, (8, LANES))
    lane = lax.broadcasted_iota(jnp.int32, (8, LANES), 1)
    step = 1
    while step < per_group:
        low = pltpu.roll(value, step, 1)
        high = pltpu.roll(value, LANES - step, 1)
        value = value + jnp.where((lane & step) != 0, low, high)
        step *= 2
    return value[0:1]


def kernel(
    n, height, width, channels,
    feat_hbm, gout_hbm, filt_hbm, gain_ref, bias_ref,
    gin_hbm, fg_ref, sums_ref,
    gin_ref, feat, gext, filt, gt, act, gact, part, r1, s2, r2, s3, r3, held, stat, sums,
    local_sem, halo_send, halo_recv, stat_send, stat_recv, sums_send, sums_recv,
    send1, recv1, send2, recv2, send3, recv3,
):
    me = lax.axis_index("rows")
    core, second, third = lax.rem(me, 2), lax.rem(lax.div(me, 2), 2), lax.div(me, 4)
    thirds = n // 4
    block = channels // n
    chunks = channels // LANES
    per_group = channels // GROUPS
    local_pixels = height * width
    pixels = local_pixels * n
    members = pixels * per_group
    taps = 9
    pieces = taps * SPLIT
    span = channels // SPLIT

    def remote(src, dst, send, recv, target):
        return pltpu.make_async_remote_copy(
            src_ref=src, dst_ref=dst, send_sem=send, recv_sem=recv,
            device_id={"rows": target}, device_id_type=MESH,
        )

    def peer(k):
        return lax.rem(me + k, n)

    in_feat = pltpu.make_async_copy(feat_hbm, feat, local_sem.at[0])
    in_gout = pltpu.make_async_copy(
        gout_hbm, gext.at[pl.ds(width, local_pixels)], local_sem.at[1]
    )
    in_filt = pltpu.make_async_copy(filt_hbm, filt, local_sem.at[2])
    in_feat.start()
    in_gout.start()

    barrier = pltpu.get_barrier_semaphore()

    def greet(k, carry):
        pl.semaphore_signal(barrier, inc=1, device_id={"rows": peer(k)}, device_id_type=MESH)
        return carry

    lax.fori_loop(1, n, greet, 0)

    lane = lax.broadcasted_iota(jnp.int32, (1, LANES), 1)
    slot = lane & (per_group - 1)
    in_feat.wait()
    in_gout.wait()
    in_filt.start()

    packed = jnp.zeros((1, LANES), F32)
    largest = jnp.zeros((16, LANES), BF16)
    for c in range(chunks):
        cols = slice(c * LANES, (c + 1) * LANES)

        def stats_step(h, carry):
            total, square, top = carry
            x = feat[pl.ds(h * width, width), cols].astype(F32)
            g = jnp.abs(gext[pl.ds((h + 1) * width, width), cols])
            x = x.reshape(width // 8, 8, LANES)
            g = g.reshape(width // 16, 16, LANES)
            return (
                total + x.sum(0), square + (x * x).sum(0), jnp.maximum(top, g.max(0))
            )

        zero = jnp.zeros((8, LANES), F32)
        total, square, largest = lax.fori_loop(0, height, stats_step, (zero, zero, largest))
        total = group_sum(total.sum(0, keepdims=True), per_group)
        square = group_sum(square.sum(0, keepdims=True), per_group)
        packed = packed + jnp.where(slot == c, total, 0.0)
        packed = packed + jnp.where(slot == chunks + c, square, 0.0)
    top = jnp.max(largest.astype(F32).max(0, keepdims=True), axis=1, keepdims=True)
    is_top = slot == 2 * chunks
    stat[me] = packed + jnp.where(is_top, top, 0.0)

    pl.semaphore_wait(barrier, n - 1)

    def stat_copy(k, source):
        return remote(stat.at[me], stat.at[source], stat_send.at[k], stat_recv.at[source], peer(k))

    def stat_start(k, carry):
        stat_copy(k, me).start()
        return carry

    lax.fori_loop(1, n, stat_start, 0)

    up, down = lax.rem(me + n - 1, n), lax.rem(me + 1, n)
    above, below = pl.ds(0, width), pl.ds((height + 1) * width, width)
    halo_up = remote(
        gext.at[pl.ds(width, width)], gext.at[below], halo_send.at[0], halo_recv.at[0], up
    )
    halo_down = remote(
        gext.at[pl.ds(height * width, width)], gext.at[above], halo_send.at[1], halo_recv.at[1], down
    )

    @pl.when(me > 0)
    def _():
        halo_up.start()

    @pl.when(me < n - 1)
    def _():
        halo_down.start()

    @pl.when(me == 0)
    def _():
        gext[above, :] = jnp.zeros((width, channels), BF16)

    @pl.when(me == n - 1)
    def _():
        gext[below, :] = jnp.zeros((width, channels), BF16)

    column = lax.broadcasted_iota(jnp.int32, (width, LANES), 0)

    def from_left(x):
        return jnp.where(column > 0, pltpu.roll(x, 1, 0), 0.0)

    def from_right(x):
        return jnp.where(column < width - 1, pltpu.roll(x, width - 1, 0), 0.0)

    def conv(h):
        wide = 2 * LANES
        for c in range(channels // wide):
            cols = slice(c * wide, (c + 1) * wide)
            ys = []
            for s in range(3):
                y = None
                for r in range(3):
                    rows = pl.ds(pl.multiple_of((h - r + 2) * width, width), width)
                    d = jnp.dot(
                        gext[rows, :], filt[3 * r + s, :, cols], preferred_element_type=F32
                    )
                    y = d if y is None else y + d
                ys.append(y)
            for k in range(2):
                sub = slice(k * LANES, (k + 1) * LANES)
                value = ys[1][:, sub] + from_right(ys[0][:, sub]) + from_left(ys[2][:, sub])
                gact[pl.ds(pl.multiple_of(h * width, width), width),
                     c * wide + k * LANES:c * wide + (k + 1) * LANES] = value

    def transpose(e):
        start = pl.multiple_of(e * width, width)
        gt[:, pl.ds(start, width)] = gext[pl.ds(start, width), :].T

    in_filt.wait()

    def inner(h, carry):
        conv(h)
        return carry

    lax.fori_loop(1, height - 1, inner, 0)

    def own_transposes(e, carry):
        transpose(e)
        return carry

    lax.fori_loop(1, height + 1, own_transposes, 0)

    def stat_wait(k, carry):
        stat_copy(k, peer(k)).wait_recv()
        return carry

    lax.fori_loop(1, n, stat_wait, 0)
    everyone = stat[...]
    total_stat = everyone.sum(0)
    gmax = jnp.max(
        jnp.where(is_top, everyone.max(0), 0.0), axis=1, keepdims=True
    )
    bound = GAIN_MAX * math.sqrt(float(pixels) * float(members)) + BIAS_MAX * pixels
    reach = bound * jnp.maximum(gmax, 1e-30) * (2.0 ** -13.9)
    scale = 1.0 / reach
    means, invs = [], []
    for c in range(chunks):
        total = group_sum(jnp.where(slot == c, total_stat, 0.0), per_group)
        square = group_sum(jnp.where(slot == chunks + c, total_stat, 0.0), per_group)
        mean = total / members
        means.append(mean)
        invs.append(lax.rsqrt(square / members - mean * mean + EPSILON))

    def forward(rows, c):
        cols = slice(c * LANES, (c + 1) * LANES)
        normalized = (feat[rows, cols].astype(F32) - means[c]) * invs[c]
        normed = normalized * gain_ref[:, cols] + bias_ref[:, cols]
        return normalized, normed, 1.0 / (1.0 + jnp.exp(-normed))

    def rows_of(h):
        return pl.ds(pl.multiple_of(h * width, width), width)

    def activate(h, carry):
        rows = rows_of(h)
        for c in range(chunks):
            cols = slice(c * LANES, (c + 1) * LANES)
            _, normed, sig = forward(rows, c)
            a = normed * sig
            act[0, rows, cols] = from_left(a).astype(BF16)
            act[1, rows, cols] = a.astype(BF16)
            act[2, rows, cols] = from_right(a).astype(BF16)
        return carry

    lax.fori_loop(0, height, activate, 0)

    def halo_arrived():
        @pl.when(me < n - 1)
        def _():
            halo_up.wait_recv()

        @pl.when(me > 0)
        def _():
            halo_down.wait_recv()

        transpose(0)
        transpose(height + 1)

    def copy1(t):
        target = me + 1 - 2 * core
        return remote(part.at[t, 1 - core], r1.at[t], send1.at[t], recv1.at[t], target)

    def copy2(t):
        target = me + 2 - 4 * second
        return remote(s2.at[t], r2.at[t], send2.at[t], recv2.at[t], target)

    def other(k):
        return lax.rem(third + k, thirds)

    def copy3(t, k, source):
        goal = other(k)
        return remote(
            s3.at[t, goal], r3.at[t, source], send3.at[t, k], recv3.at[t, source],
            goal * 4 + second * 2 + core,
        )

    def multiply(q):
        t = lax.div(q, SPLIT)
        r, s = lax.rem(lax.div(t, 3) + 1, 3), lax.rem(t, 3)
        start = pl.multiple_of((2 - r) * width, LANES)
        cols = pl.ds(pl.multiple_of(lax.rem(q, SPLIT) * span, LANES), span)
        half = channels // 2
        for m in range(2):
            result = jnp.dot(
                gt[m * half:(m + 1) * half, pl.ds(start, local_pixels)], act[s, :, cols],
                preferred_element_type=F32,
            )
            for b in range(n // 2):
                d = m * (n // 2) + b
                part[q, d % 2, (d // 2) % 2, d // 4] = result[b * block:(b + 1) * block]
        copy1(q).start()

    def stage2(q):
        copy1(q).wait_recv()
        for j in range(thirds):
            s2[q, j] = encode((part[q, core, 1 - second, j] + r1[q, 1 - second, j]) * scale)
        copy2(q).start()

    def stage3(q):
        copy2(q).wait_recv()

        def piece(goal):
            own = part[q, core, second, goal] + r1[q, second, goal]
            return own * scale + decode(r2[q, goal])

        for k in range(1, thirds):
            s3[q, other(k)] = encode(piece(other(k)))
            copy3(q, k, third).start()
        held[q] = piece(third)

    def stage4(q):
        total = held[q]
        for k in range(1, thirds):
            copy3(q, k, other(k)).wait_recv()
            total = total + decode(r3[q, other(k)])
        t = lax.div(q, SPLIT)
        tap = 3 * lax.rem(lax.div(t, 3) + 1, 3) + lax.rem(t, 3)
        cols = pl.ds(pl.multiple_of(lax.rem(q, SPLIT) * span, LANES), span)
        fg_ref[tap, :, cols] = total * (reach / pixels)

    lag3, lag4 = LAG3, LAG4

    def run(first, last):
        def step(q, carry):
            @pl.when(q < pieces)
            def _():
                multiply(q)

            @pl.when((q >= 1) & (q <= pieces))
            def _():
                stage2(q - 1)

            @pl.when((q >= lag3) & (q < pieces + lag3))
            def _():
                stage3(q - lag3)

            @pl.when(q >= lag4)
            def _():
                stage4(q - lag4)

            return carry

        lax.fori_loop(first, last, step, 0)

    run(0, 4)
    halo_arrived()
    conv(0)
    run(4, 6)
    if height > 1:
        conv(height - 1)
    run(6, 8)

    for c in range(chunks):
        cols = slice(c * LANES, (c + 1) * LANES)

        def grad_step(h, carry):
            bias_sum, gain_sum = carry
            rows = rows_of(h)
            normalized, normed, sig = forward(rows, c)
            pre = gact[rows, cols] * (sig * (1.0 + normed * (1.0 - sig)))
            gact[rows, cols] = pre
            return (
                bias_sum + pre.reshape(width // 8, 8, LANES).sum(0),
                gain_sum + (pre * normalized).reshape(width // 8, 8, LANES).sum(0),
            )

        zero = jnp.zeros((8, LANES), F32)
        bias_sum, gain_sum = lax.fori_loop(0, height, grad_step, (zero, zero))
        sums[me, c:c + 1, :] = bias_sum.sum(0, keepdims=True)
        sums[me, chunks + c:chunks + c + 1, :] = gain_sum.sum(0, keepdims=True)

    def sums_copy(k, source):
        return remote(sums.at[me], sums.at[source], sums_send.at[k], sums_recv.at[source], peer(k))

    def sums_start(k, carry):
        sums_copy(k, me).start()
        return carry

    lax.fori_loop(1, n, sums_start, 0)

    run(8, pieces + 1)

    def sums_wait(k, carry):
        sums_copy(k, peer(k)).wait_recv()
        return carry

    lax.fori_loop(1, n, sums_wait, 0)
    all_sums = sums[...].sum(0)
    sums_ref[...] = all_sums
    for c in range(chunks):
        cols = slice(c * LANES, (c + 1) * LANES)
        gain = gain_ref[:, cols]
        mean_grad = group_sum(gain * all_sums[c:c + 1], per_group) / members
        mean_cross = group_sum(gain * all_sums[chunks + c:chunks + c + 1], per_group) / members

        def final_step(h, carry):
            rows = rows_of(h)
            normalized = (feat[rows, cols].astype(F32) - means[c]) * invs[c]
            result = invs[c] * (gact[rows, cols] * gain - mean_grad - normalized * mean_cross)
            gin_ref[rows, cols] = result.astype(BF16)
            return carry

        lax.fori_loop(0, height, final_step, 0)

    out_gin = pltpu.make_async_copy(gin_ref, gin_hbm, local_sem.at[3])
    out_gin.start()
    run(pieces + 1, pieces + lag4)

    def drain(q, carry):
        copy1(q).wait_send()
        copy2(q).wait_send()
        for k in range(1, thirds):
            copy3(q, k, third).wait_send()
        return carry

    lax.fori_loop(0, pieces, drain, 0)
    out_gin.wait()

    def small_sends(k, carry):
        stat_copy(k, me).wait_send()
        sums_copy(k, me).wait_send()
        return carry

    lax.fori_loop(1, n, small_sends, 0)

    @pl.when(me > 0)
    def _():
        halo_up.wait_send()

    @pl.when(me < n - 1)
    def _():
        halo_down.wait_send()


def hand_over(gin, fg, sums, gin_out, fg_out, gain_out, bias_out, sem):
    first = pltpu.make_async_copy(gin, gin_out, sem.at[0])
    second = pltpu.make_async_copy(fg, fg_out, sem.at[1])
    first.start()
    second.start()
    chunks = sums.shape[0] // 2
    for c in range(chunks):
        cols = slice(c * LANES, (c + 1) * LANES)
        bias_out[:, cols] = sums[c:c + 1, :]
        gain_out[:, cols] = sums[chunks + c:chunks + c + 1, :]
    first.wait()
    second.wait()


def local(n, features, grad_out, filters, norm_gain, norm_bias):
    height, width, channels = features.shape
    pixels = height * width
    block, thirds, chunks = channels // n, n // 4, channels // LANES
    taps = 9
    pieces, span = taps * SPLIT, channels // SPLIT
    by_tap = filters.transpose(1, 2, 0, 3).reshape(taps, channels, channels)
    dma = pltpu.SemaphoreType.DMA
    grad_in, filter_grad, sums = pl.pallas_call(
        functools.partial(kernel, n, height, width, channels),
        out_shape=(
            jax.ShapeDtypeStruct((pixels, channels), BF16),
            jax.ShapeDtypeStruct((taps, block, channels), F32),
            jax.ShapeDtypeStruct((2 * chunks, LANES), F32),
        ),
        in_specs=[pl.BlockSpec(memory_space=pl.ANY)] * 3
        + [pl.BlockSpec(memory_space=pltpu.VMEM)] * 2,
        out_specs=(
            pl.BlockSpec(memory_space=pl.ANY),
            pl.BlockSpec(memory_space=pltpu.VMEM),
            pl.BlockSpec(memory_space=pltpu.VMEM),
        ),
        scratch_shapes=[
            pltpu.VMEM((pixels, channels), BF16),
            pltpu.VMEM((pixels, channels), BF16),
            pltpu.VMEM((pixels + 2 * width, channels), BF16),
            pltpu.VMEM((taps, channels, channels), BF16),
            pltpu.VMEM((channels, pixels + 2 * width), BF16),
            pltpu.VMEM((3, pixels, channels), BF16),
            pltpu.VMEM((pixels, channels), F32),
            pltpu.VMEM((pieces, 2, 2, thirds, block, span), F32),
            pltpu.VMEM((pieces, 2, thirds, block, span), F32),
            pltpu.VMEM((pieces, thirds, block, span), BF16),
            pltpu.VMEM((pieces, thirds, block, span), BF16),
            pltpu.VMEM((pieces, thirds, block, span), BF16),
            pltpu.VMEM((pieces, thirds, block, span), BF16),
            pltpu.VMEM((pieces, block, span), F32),
            pltpu.VMEM((n, 1, LANES), F32),
            pltpu.VMEM((n, 2 * chunks, LANES), F32),
            dma((4,)), dma((2,)), dma((2,)),
            dma((n,)), dma((n,)), dma((n,)), dma((n,)),
            dma((pieces,)), dma((pieces,)), dma((pieces,)), dma((pieces,)),
            dma((pieces, thirds)), dma((pieces, thirds)),
        ],
        compiler_params=pltpu.CompilerParams(
            collective_id=0, has_side_effects=True, vmem_limit_bytes=MAIN * 1024 * 1024
        ),
        name="block_backward",
    )(
        features.reshape(pixels, channels), grad_out.reshape(pixels, channels), by_tap,
        norm_gain.reshape(1, channels), norm_bias.reshape(1, channels),
    )
    any_space, vmem = pl.BlockSpec(memory_space=pl.ANY), pl.BlockSpec(memory_space=pltpu.VMEM)
    grad_in, filter_grad, gain_grad, bias_grad = pl.pallas_call(
        hand_over,
        out_shape=(
            jax.ShapeDtypeStruct((pixels, channels), BF16),
            jax.ShapeDtypeStruct((taps, block, channels), F32),
            jax.ShapeDtypeStruct((1, channels), F32),
            jax.ShapeDtypeStruct((1, channels), F32),
        ),
        in_specs=[vmem, vmem, vmem],
        out_specs=(any_space, any_space, vmem, vmem),
        scratch_shapes=[dma((2,))],
        compiler_params=pltpu.CompilerParams(vmem_limit_bytes=8 * 1024 * 1024),
        name="hand_over",
    )(grad_in, filter_grad, sums)
    return (
        grad_in.reshape(height, width, channels),
        filter_grad.transpose(1, 0, 2).reshape(block, 3, 3, channels),
        gain_grad.reshape(channels),
        bias_grad.reshape(channels),
    )


def solution(mesh):
    slabs = P(("parts", "rows"), None, None)
    return jax.shard_map(
        functools.partial(local, mesh.shape["rows"]),
        mesh=mesh,
        in_specs=(slabs, slabs, P(), P(), P()),
        out_specs=(slabs, P(("parts", "rows"), None, None, None), P("parts"), P("parts")),
        check_vma=False,
    )
```

profile of v0, /device:TPU:0, one launch (start us, length us, event | category | flops | bytes accessed | tf_op | source)
XLA Modules:
  0.0 57.2 jit_solution(8587941290226728932)
XLA Ops:
  0.6 51.9 %block_backward.1 = (bf16[1024,512]{1,0:T(8,128)(2,1)}, f32[9,32,512]{2,1,0:T(8,128)}, f32[8,128]{1,0:T(8,128)}) custom-call(bf16[1024,512]{1,0:T(8,128)(2,1)} %bitcast.14, bf16[1024,512]{1,0:T(8,128)(2,1)} %bitcast.15, bf16[9,512,512]{2,1,0:T(8,128)(2,1)} %bitcast.13, f32[1,512]{1,0:T(1,128)} %bitcast.16, f32[1,512]{1,0:T(1,128)} %bitcast.17), custom_call_target="tpu_custom_call" | custom-call | tf_op jit(solution)/shard_map/block_backward/pallas_call | solution.py:463
  52.5 0.0 copy-start
  52.5 1.2 %copy-done = bf16[1024,512]{1,0:T(8,128)(2,1)S(1)} copy-done((bf16[1024,512]{1,0:T(8,128)(2,1)S(1)}, bf16[1024,512]{1,0:T(8,128)(2,1)}, u32[]{:S(2)}) %copy-start) | copy-done | bytes 1048600
  53.7 0.0 copy-start.1
  53.7 1.1 %copy-done.1 = f32[9,32,512]{2,1,0:T(8,128)S(1)} copy-done((f32[9,32,512]{2,1,0:T(8,128)S(1)}, f32[9,32,512]{2,1,0:T(8,128)}, u32[]{:S(2)}) %copy-start.1) | copy-done | bytes 589848
  54.8 0.0 copy-start.2
  54.8 0.7 %copy-done.2 = f32[8,128]{1,0:T(8,128)S(1)} copy-done((f32[8,128]{1,0:T(8,128)S(1)}, f32[8,128]{1,0:T(8,128)}, u32[]{:S(2)}) %copy-start.2) | copy-done | bytes 4120
  55.5 1.8 %hand_over.1 = (bf16[1024,512]{1,0:T(8,128)(2,1)}, f32[9,32,512]{2,1,0:T(8,128)}, f32[1,512]{1,0:T(1,128)}, f32[1,512]{1,0:T(1,128)}) custom-call(bf16[1024,512]{1,0:T(8,128)(2,1)S(1)} %copy-done, f32[9,32,512]{2,1,0:T(8,128)S(1)} %copy-done.1, f32[8,128]{1,0:T(8,128)S(1)} %copy-done.2), custom_call_target="tpu_custom_call" | custom-call | tf_op jit(solution)/shard_map/hand_over/pallas_call | solution.py:508
Async XLA Ops:
  52.5 1.2 %copy-start = (bf16[1024,512]{1,0:T(8,128)(2,1)S(1)}, bf16[1024,512]{1,0:T(8,128)(2,1)}, u32[]{:S(2)}) copy-start(bf16[1024,512]{1,0:T(8,128)(2,1)} %get-tuple-element.11.gin) | copy-start | bytes 3145732
  53.7 1.1 %copy-start.1 = (f32[9,32,512]{2,1,0:T(8,128)S(1)}, f32[9,32,512]{2,1,0:T(8,128)}, u32[]{:S(2)}) copy-start(f32[9,32,512]{2,1,0:T(8,128)} %get-tuple-element.12.fg) | copy-start | bytes 1769476
  54.8 0.7 %copy-start.2 = (f32[8,128]{1,0:T(8,128)S(1)}, f32[8,128]{1,0:T(8,128)}, u32[]{:S(2)}) copy-start(f32[8,128]{1,0:T(8,128)} %get-tuple-element.13.sums) | copy-start | bytes 12292
where the time goes:
time: 57.5 us; the launch traced here: 57.2 us
  Pallas kernels  53.6 us (93%)
  local copies, waits for them, and re-layouts  2.96 us (5%)
  between operations  0.65 us (1%)
    pallas_call x1, Pallas kernels, local(): pl.pallas_call(functools.partial(kernel, n, height, width, channels), out...  51.9 us
    unnamed x6, local copies, waits for them, and re-layouts  2.96 us
    pallas_call x1, Pallas kernels, local(): pl.pallas_call(hand_over, out_shape=(jax.ShapeDtypeStruct((pixels, channe...  1.76 us

commit v1 on v0

v1 whole, which is shorter than its diff:
```python
import functools
import math

import jax
import jax.numpy as jnp
from jax import lax
from jax.experimental import pallas as pl
from jax.experimental.pallas import tpu as pltpu
from jax.sharding import PartitionSpec as P

GROUPS = 32
LANES = 128
POWER = 9
TAPS = 9
LAG_B = 2
MAIN = 40
EPSILON = 1e-06
GAIN_MAX = 1.75
BIAS_MAX = 1.0
MESH = pl.DeviceIdType.MESH
F32 = jnp.float32
BF16 = jnp.bfloat16


def encode(value):
    square = value * value
    fourth = square * square
    return (fourth * fourth * value).astype(BF16)


def decode(coded):
    wide = coded.astype(F32)
    root = jnp.exp2(jnp.log2(jnp.maximum(jnp.abs(wide), 1e-38)) * (1.0 / POWER))
    root = jnp.where(jnp.abs(wide) < 1e-37, 0.0, root)
    return jnp.where(wide < 0.0, -root, root)


def group_sum(row, per_group):
    value = jnp.broadcast_to(row, (8, LANES))
    lane = lax.broadcasted_iota(jnp.int32, (8, LANES), 1)
    step = 1
    while step < per_group:
        low = pltpu.roll(value, step, 1)
        high = pltpu.roll(value, LANES - step, 1)
        value = value + jnp.where((lane & step) != 0, low, high)
        step *= 2
    return value[0:1]


def kernel(
    n, height, width, channels,
    feat_hbm, gout_hbm, filt_hbm, gain_hbm, bias_hbm,
    gin_ref, fg_ref, sums_ref,
    feat, featc, gext, filt, gt, act, gact, part, sa, ra, sb, rb, sm, rm, sc, rc, hs, hr,
    gin_s, gin_r, stat, tops, sums, gain_ref, bias_ref,
    feat_sem, local_sem, push_send, push_recv, halo_send, halo_recv,
    stat_send, stat_recv, tops_send, tops_recv, sums_send, sums_recv,
    a_send, a_recv, b_send, b_recv, m_send, m_recv, c_send, c_recv, h_send, h_recv,
):
    me = lax.axis_index("rows")
    core, chip = lax.rem(me, 2), lax.div(me, 2)
    mate = me + 1 - 2 * core
    chips = n // 2
    bits = chips.bit_length() - 1
    bit = [lax.rem(lax.div(chip, 1 << j), 2) for j in range(bits)]
    across = [(2 << j) * (1 - 2 * bit[j]) for j in range(bits)]
    block = channels // n
    half = channels // 2
    chunks = channels // LANES
    mine = half // LANES
    per_group = channels // GROUPS
    slab = height * width
    tall = 2 * height
    area = 2 * slab
    pixels = slab * n
    members = pixels * per_group
    own = pl.multiple_of(core * slab, slab)
    other = pl.multiple_of((1 - core) * slab, slab)
    my_cols = pl.multiple_of(core * half, LANES)
    mate_cols = pl.multiple_of((1 - core) * half, LANES)

    def remote(src, dst, send, recv, target):
        return pltpu.make_async_remote_copy(
            src_ref=src, dst_ref=dst, send_sem=send, recv_sem=recv,
            device_id={"rows": target}, device_id_type=MESH,
        )

    def peer(k):
        return lax.rem(me + k, n)

    def rows_of(h):
        return pl.ds(pl.multiple_of(h * width, width), width)

    in_feat = [
        pltpu.make_async_copy(
            feat_hbm.at[pl.ds(h * width, width)], feat.at[pl.ds(h * width, width)], feat_sem.at[h]
        )
        for h in range(height)
    ]
    in_gout = pltpu.make_async_copy(
        gout_hbm, gext.at[pl.ds(width + own, slab)], local_sem.at[0]
    )
    in_half = pltpu.make_async_copy(
        feat_hbm.at[:, pl.ds(my_cols, half)], featc.at[pl.ds(own, slab)], local_sem.at[1]
    )
    in_filt = pltpu.make_async_copy(
        filt_hbm.at[:, :, pl.ds(my_cols, half)], filt, local_sem.at[2]
    )
    in_gain = pltpu.make_async_copy(gain_hbm, gain_ref, local_sem.at[3])
    in_bias = pltpu.make_async_copy(bias_hbm, bias_ref, local_sem.at[4])
    for copy in in_feat:
        copy.start()
    in_gout.start()
    in_half.start()
    in_filt.start()
    in_gain.start()
    in_bias.start()

    barrier = pltpu.get_barrier_semaphore()

    def greet(k, carry):
        pl.semaphore_signal(barrier, inc=1, device_id={"rows": peer(k)}, device_id_type=MESH)
        return carry

    lax.fori_loop(1, n, greet, 0)

    def shared(buffer, send, recv):
        def copy(k, source):
            return remote(buffer.at[me], buffer.at[source], send.at[k], recv.at[source], peer(k))

        def start():
            def body(k, carry):
                copy(k, me).start()
                return carry
            lax.fori_loop(1, n, body, 0)

        def wait():
            def body(k, carry):
                copy(k, peer(k)).wait_recv()
                return carry
            lax.fori_loop(1, n, body, 0)

        def drain():
            def body(k, carry):
                copy(k, me).wait_send()
                return carry
            lax.fori_loop(1, n, body, 0)

        return start, wait, drain

    stat_start, stat_wait, stat_drain = shared(stat, stat_send, stat_recv)
    tops_start, tops_wait, tops_drain = shared(tops, tops_send, tops_recv)
    sums_start, sums_wait, sums_drain = shared(sums, sums_send, sums_recv)

    lane = lax.broadcasted_iota(jnp.int32, (1, LANES), 1)
    slot = lane & (per_group - 1)
    totals = [jnp.zeros((8, LANES), F32) for _ in range(chunks)]
    squares = [jnp.zeros((8, LANES), F32) for _ in range(chunks)]
    for h in range(height):
        in_feat[h].wait()
        for c in range(chunks):
            x = feat[h * width:(h + 1) * width, c * LANES:(c + 1) * LANES].astype(F32)
            x = x.reshape(width // 8, 8, LANES)
            totals[c] = totals[c] + x.sum(0)
            squares[c] = squares[c] + (x * x).sum(0)
    packed = jnp.zeros((1, LANES), F32)
    for c in range(chunks):
        total = group_sum(totals[c].sum(0, keepdims=True), per_group)
        square = group_sum(squares[c].sum(0, keepdims=True), per_group)
        packed = packed + jnp.where(slot == c, total, 0.0)
        packed = packed + jnp.where(slot == chunks + c, square, 0.0)
    stat[me] = packed

    pl.semaphore_wait(barrier, n - 1)
    stat_start()

    push_feat = remote(
        feat.at[:, pl.ds(mate_cols, half)], featc.at[pl.ds(own, slab)],
        push_send.at[0], push_recv.at[0], mate,
    )
    push_gout = remote(
        gext.at[pl.ds(width + own, slab)], gext.at[pl.ds(width + own, slab)],
        push_send.at[1], push_recv.at[1], mate,
    )
    push_feat.start()
    in_gout.wait()
    push_gout.start()

    above, below = pl.ds(0, width), pl.ds((tall + 1) * width, width)
    first, last = pl.ds(width, width), pl.ds(tall * width, width)

    def to_above(k):
        return remote(gext.at[first], gext.at[below], halo_send.at[k], halo_recv.at[0], me - 1 - k)

    def to_below(k):
        return remote(gext.at[last], gext.at[above], halo_send.at[k], halo_recv.at[1], me + 1 + k)

    has_above, has_below = chip > 0, chip < chips - 1

    @pl.when((core == 0) & has_above)
    def _():
        to_above(0).start()
        to_above(1).start()

    @pl.when((core == 1) & has_below)
    def _():
        to_below(0).start()
        to_below(1).start()

    @pl.when(chip == 0)
    def _():
        gext[above, :] = jnp.zeros((width, channels), BF16)

    @pl.when(chip == chips - 1)
    def _():
        gext[below, :] = jnp.zeros((width, channels), BF16)

    def top_step(h, carry):
        g = jnp.abs(gext[rows_of(1 + core * height + h), :])
        return jnp.maximum(carry, g.reshape(width // 16, 16, channels).max(0))

    largest = lax.fori_loop(0, height, top_step, jnp.zeros((16, channels), BF16))
    largest = largest.astype(F32).max(0, keepdims=True)
    top = jnp.zeros((1, LANES), F32)
    for c in range(chunks):
        top = jnp.maximum(top, largest[:, c * LANES:(c + 1) * LANES])
    tops[me] = top
    tops_start()

    column = lax.broadcasted_iota(jnp.int32, (width, LANES), 0)

    def from_left(x):
        return jnp.where(column > 0, pltpu.roll(x, 1, 0), 0.0)

    def from_right(x):
        return jnp.where(column < width - 1, pltpu.roll(x, width - 1, 0), 0.0)

    def conv(j):
        first_row = lax.rem(core * height + 1 + 2 * j, tall)
        where = [first_row, lax.rem(first_row + 1, tall)]
        ys = [[], []]
        for s in range(3):
            for m in range(2):
                y = None
                for r in range(3):
                    d = jnp.dot(
                        gext[rows_of(where[m] - r + 2), :], filt[3 * r + s],
                        preferred_element_type=F32,
                    )
                    y = d if y is None else y + d
                ys[m].append(y)
        for m in range(2):
            for k in range(mine):
                sub = slice(k * LANES, (k + 1) * LANES)
                y = ys[m]
                gact[rows_of(where[m]), sub] = (
                    y[1][:, sub] + from_right(y[0][:, sub]) + from_left(y[2][:, sub])
                )

    def transpose(e):
        start = pl.multiple_of(e * width, width)
        gt[:, pl.ds(start, width)] = gext[pl.ds(start, width), :].T

    def transposes(base, count):
        def body(e, carry):
            transpose(base + e)
            return carry
        lax.fori_loop(0, count, body, 0)

    transposes(1 + core * height, height)
    in_filt.wait()
    if height >= 4:
        conv(0)

    push_gout_in = remote(
        gext.at[pl.ds(width + other, slab)], gext.at[pl.ds(width + other, slab)],
        push_send.at[1], push_recv.at[1], mate,
    )
    push_feat_in = remote(
        feat.at[:, pl.ds(mate_cols, half)], featc.at[pl.ds(other, slab)],
        push_send.at[0], push_recv.at[0], mate,
    )
    push_gout_in.wait_recv()
    transposes(1 + (1 - core) * height, height)

    @pl.when(has_below)
    def _():
        to_above(0).wait_recv()

    @pl.when(has_above)
    def _():
        to_below(0).wait_recv()

    transpose(0)
    transpose(tall + 1)
    if height < 4:
        conv(0)
    conv(1)
    in_half.wait()
    in_gain.wait()
    in_bias.wait()
    push_feat_in.wait_recv()

    stat_wait()
    total_stat = stat[...].sum(0)
    means, invs, gains, biases = [], [], [], []
    for k in range(mine):
        which = core * mine + k
        total = group_sum(jnp.where(slot == which, total_stat, 0.0), per_group)
        square = group_sum(jnp.where(slot == chunks + which, total_stat, 0.0), per_group)
        mean = total / members
        means.append(mean)
        invs.append(lax.rsqrt(square / members - mean * mean + EPSILON))
        at = pl.ds(pl.multiple_of(my_cols + k * LANES, LANES), LANES)
        gains.append(gain_ref[:, at])
        biases.append(bias_ref[:, at])

    def forward(rows, k):
        cols = slice(k * LANES, (k + 1) * LANES)
        normalized = (featc[rows, cols].astype(F32) - means[k]) * invs[k]
        normed = normalized * gains[k] + biases[k]
        return normalized, normed, 1.0 / (1.0 + jnp.exp(-normed))

    def activate(h, carry):
        rows = rows_of(h)
        for k in range(mine):
            _, normed, sig = forward(rows, k)
            act[1, rows, k * LANES:(k + 1) * LANES] = (normed * sig).astype(BF16)
        return carry

    lax.fori_loop(0, tall, activate, 0)

    tops_wait()
    gmax = jnp.max(tops[...].max(0), axis=1, keepdims=True)
    bound = GAIN_MAX * math.sqrt(float(pixels) * float(members)) + BIAS_MAX * pixels
    reach = bound * jnp.maximum(gmax, 1e-30) * (2.0 ** -13.9)
    scale = 1.0 / reach

    def shift(h, carry):
        rows = rows_of(h)
        for k in range(mine):
            cols = slice(k * LANES, (k + 1) * LANES)
            a = act[1, rows, cols].astype(F32)
            act[0, rows, cols] = from_left(a).astype(BF16)
            act[2, rows, cols] = from_right(a).astype(BF16)
        return carry

    def multiply(t):
        s = lax.rem(1 + 2 * lax.div(t, 3), 3)
        start = pl.multiple_of((2 - lax.rem(t, 3)) * width, LANES)
        for m in range(2):
            result = jnp.dot(
                gt[m * half:(m + 1) * half, pl.ds(start, area)], act[s],
                preferred_element_type=F32,
            )
            part[t, m * (chips // 2):(m + 1) * (chips // 2)] = result.reshape(
                chips // 2, 2 * block, half
            )

    def swapped(t, k):
        return (1 - lax.rem(t, 2)) * k

    def pair_delta(kind):
        return kind * across[1] + (1 - kind) * across[0]

    def copy_a(t, k):
        target = me + pair_delta(swapped(t, k))
        return remote(sa.at[t, k], ra.at[t, k], a_send.at[t, k], a_recv.at[t, k], target)

    def copy_b(t, k):
        target = me + pair_delta(1 - swapped(t, k))
        return remote(sb.at[t, k], rb.at[t, k], b_send.at[t, k], b_recv.at[t, k], target)

    def copy_m(t, k, j):
        at = pl.ds(chips // 4 - (chips >> j), chips >> (j + 1))
        return remote(
            sm.at[t, k, at], rm.at[t, k, at],
            m_send.at[t, k, j], m_recv.at[t, k, j], me + across[j],
        )

    def copy_c(t, k, way, source):
        target = lax.div(me + across[bits - 1], 2) * 2 + way
        return remote(
            sc.at[t, k, way], rc.at[t, k, source],
            c_send.at[t, k, way], c_recv.at[t, k, source], target,
        )

    def copy_h(t, k):
        return remote(hs.at[t, k], hr.at[t, k], h_send.at[t, k], h_recv.at[t, k], mate)

    def lanes_of(k):
        return slice(k * LANES, (k + 1) * LANES)

    def stage_a(t, k):
        kind = swapped(t, k)
        for w in range(chips // 2):
            u, v = w >> 1, w & 1
            dest = u * 4 + kind * (2 * (1 - bit[1]) + v) + (1 - kind) * (2 * v + 1 - bit[0])
            sa[t, k, w] = encode(part[t, dest, :, lanes_of(k)] * scale)
        copy_a(t, k).start()

    def stage_b(t, k):
        copy_a(t, k).wait_recv()
        kind = swapped(t, k)
        mine_bit = kind * bit[0] + (1 - kind) * bit[1]

        def value(u, v):
            dest = u * 4 + kind * (2 * bit[1] + v) + (1 - kind) * (2 * v + bit[0])
            return part[t, dest, :, lanes_of(k)] * scale + decode(ra[t, k, 2 * u + v])

        for u in range(chips // 4):
            sb[t, k, u] = encode(value(u, 1 - mine_bit))
        copy_b(t, k).start()
        for u in range(chips // 4):
            part[t, u * 4 + 2 * bit[1] + bit[0], :, lanes_of(k)] = value(u, mine_bit)

    def low(j):
        return lax.rem(chip, 1 << j)

    def received(t, k, j):
        if j == 2:
            copy_b(t, k).wait_recv()
            return rb, 0
        copy_m(t, k, j - 1).wait_recv()
        return rm, chips // 4 - (chips >> (j - 1))

    def stage_m(t, k, j):
        buffer, base = received(t, k, j)

        def value(r, side):
            coded = buffer[t, k, base + 2 * r + side]
            return part[t, (2 * r + side) * (1 << j) + low(j), :, lanes_of(k)] + decode(coded)

        for r in range(chips >> (j + 1)):
            sm[t, k, chips // 4 - (chips >> j) + r] = encode(value(r, 1 - bit[j]))
        copy_m(t, k, j).start()
        for r in range(chips >> (j + 1)):
            part[t, (2 * r + bit[j]) * (1 << j) + low(j), :, lanes_of(k)] = value(r, bit[j])

    def stage_c(t, k):
        j = bits - 1
        buffer, base = received(t, k, j)

        def value(side, rows):
            coded = buffer[t, k, base + side, rows]
            return part[t, side * (1 << j) + low(j), rows, lanes_of(k)] + decode(coded)

        for way in range(2):
            rows = slice(way * block, (way + 1) * block)
            sc[t, k, way] = encode(value(1 - bit[j], rows))
            copy_c(t, k, way, core).start()
        hs[t, k] = value(bit[j], pl.ds(pl.multiple_of((1 - core) * block, block), block))
        copy_h(t, k).start()
        rows = pl.ds(pl.multiple_of(core * block, block), block)
        part[t, chip, rows, lanes_of(k)] = value(bit[j], rows)

    def stage_d(t, k):
        tap = 3 * lax.rem(t, 3) + lax.rem(1 + 2 * lax.div(t, 3), 3)
        rows = pl.ds(pl.multiple_of(core * block, block), block)
        copy_c(t, k, core, core).wait_recv()
        total = part[t, chip, rows, lanes_of(k)]
        total = total + decode(rc[t, k, core])
        at = pl.ds(pl.multiple_of(my_cols + k * LANES, LANES), LANES)
        fg_ref[tap, :, at] = total * (reach / pixels)
        copy_h(t, k).wait_recv()
        copy_c(t, k, core, 1 - core).wait_recv()
        total = hr[t, k] + decode(rc[t, k, 1 - core])
        at = pl.ds(pl.multiple_of(mate_cols + k * LANES, LANES), LANES)
        fg_ref[tap, :, at] = total * (reach / pixels)

    def gradients():
        for k in range(mine):
            cols = lanes_of(k)

            def grad_step(h, carry):
                bias_sum, gain_sum = carry
                rows = rows_of(h)
                normalized, normed, sig = forward(rows, k)
                pre = gact[rows, cols] * (sig * (1.0 + normed * (1.0 - sig)))
                gact[rows, cols] = pre
                return (
                    bias_sum + pre.reshape(width // 8, 8, LANES).sum(0),
                    gain_sum + (pre * normalized).reshape(width // 8, 8, LANES).sum(0),
                )

            zero = jnp.zeros((8, LANES), F32)
            bias_sum, gain_sum = lax.fori_loop(0, tall, grad_step, (zero, zero))
            sums[me, k:k + 1, :] = bias_sum.sum(0, keepdims=True)
            sums[me, mine + k:mine + k + 1, :] = gain_sum.sum(0, keepdims=True)
        sums_start()

    push_gin = remote(gin_s, gin_r, push_send.at[2], push_recv.at[2], mate)

    def finish():
        sums_wait()
        everyone = sums[...].reshape(chips, 2, 2 * mine, LANES).sum(0)
        for c in range(2):
            for k in range(mine):
                sums_ref[c * mine + k:c * mine + k + 1, :] = everyone[c, k:k + 1]
                sums_ref[chunks + c * mine + k:chunks + c * mine + k + 1, :] = (
                    everyone[c, mine + k:mine + k + 1]
                )
        for side in (1, 0):
            base = (1 - core if side else core) * height
            for k in range(mine):
                mean_grad = group_sum(
                    gains[k] * sums_ref[pl.ds(core * mine + k, 1), :], per_group
                ) / members
                mean_cross = group_sum(
                    gains[k] * sums_ref[pl.ds(chunks + core * mine + k, 1), :], per_group
                ) / members
                at = pl.ds(pl.multiple_of(my_cols + k * LANES, LANES), LANES)

                def final_step(h, carry):
                    rows = rows_of(base + h)
                    cols = lanes_of(k)
                    normalized = (featc[rows, cols].astype(F32) - means[k]) * invs[k]
                    result = invs[k] * (gact[rows, cols] * gains[k] - mean_grad - normalized * mean_cross)
                    if side:
                        gin_s[rows_of(h), cols] = result.astype(BF16)
                    else:
                        gin_ref[rows_of(h), at] = result.astype(BF16)
                    return carry

                lax.fori_loop(0, height, final_step, 0)
            if side:
                push_gin.start()

    lag_d = LAG_B + bits - 1

    def run(t, carry):
        @pl.when(t < TAPS)
        def _():
            multiply(t)
            for k in range(mine):
                stage_a(t, k)

        @pl.when(t == 0)
        def _():
            lax.fori_loop(0, tall, shift, 0)

        @pl.when((t >= 1) & (t < height - 1))
        def _():
            conv(t + 1)

        @pl.when(t == 3)
        def _():
            gradients()

        @pl.when(t == 6)
        def _():
            finish()

        @pl.when((t >= LAG_B) & (t < TAPS + LAG_B))
        def _():
            for k in range(mine):
                stage_b(t - LAG_B, k)

        for j in range(2, bits - 1):
            @pl.when((t >= LAG_B + j - 1) & (t < TAPS + LAG_B + j - 1))
            def _():
                for k in range(mine):
                    stage_m(t - LAG_B - j + 1, k, j)

        @pl.when((t >= lag_d - 1) & (t < TAPS + lag_d - 1))
        def _():
            for k in range(mine):
                stage_c(t - lag_d + 1, k)

        @pl.when(t >= lag_d)
        def _():
            for k in range(mine):
                stage_d(t - lag_d, k)

        return carry

    lax.fori_loop(0, TAPS + lag_d, run, 0)

    push_gin.wait_recv()

    def collect(h, carry):
        gin_ref[rows_of(h), pl.ds(mate_cols, half)] = gin_r[rows_of(h), :]
        return carry

    lax.fori_loop(0, height, collect, 0)

    def drain(t, carry):
        for k in range(mine):
            copy_a(t, k).wait_send()
            copy_b(t, k).wait_send()
            for j in range(2, bits - 1):
                copy_m(t, k, j).wait_send()
            for way in range(2):
                copy_c(t, k, way, core).wait_send()
            copy_h(t, k).wait_send()
        return carry

    lax.fori_loop(0, TAPS, drain, 0)
    push_feat.wait_send()
    push_gout.wait_send()
    push_gin.wait_send()
    stat_drain()
    tops_drain()
    sums_drain()

    @pl.when((core == 0) & has_above)
    def _():
        to_above(0).wait_send()
        to_above(1).wait_send()

    @pl.when((core == 1) & has_below)
    def _():
        to_below(0).wait_send()
        to_below(1).wait_send()


def hand_over(gin, fg, sums, gin_out, fg_out, gain_out, bias_out, sem):
    first = pltpu.make_async_copy(gin, gin_out, sem.at[0])
    second = pltpu.make_async_copy(fg, fg_out, sem.at[1])
    first.start()
    second.start()
    chunks = sums.shape[0] // 2
    for c in range(chunks):
        cols = slice(c * LANES, (c + 1) * LANES)
        bias_out[:, cols] = sums[c:c + 1, :]
        gain_out[:, cols] = sums[chunks + c:chunks + c + 1, :]
    first.wait()
    second.wait()


def local(n, features, grad_out, filters, norm_gain, norm_bias):
    height, width, channels = features.shape
    slab = height * width
    area, half = 2 * slab, channels // 2
    block, chips, chunks = channels // n, n // 2, channels // LANES
    mine = chunks // 2
    by_tap = filters.transpose(1, 2, 0, 3).reshape(TAPS, channels, channels)
    dma = pltpu.SemaphoreType.DMA
    hbm, vmem = pl.BlockSpec(memory_space=pltpu.HBM), pl.BlockSpec(memory_space=pltpu.VMEM)
    lots = dma((TAPS, mine))
    bits, middle = chips.bit_length() - 1, max(1, chips // 4 - 2)
    grad_in, filter_grad, sums = pl.pallas_call(
        functools.partial(kernel, n, height, width, channels),
        out_shape=(
            jax.ShapeDtypeStruct((slab, channels), BF16),
            jax.ShapeDtypeStruct((TAPS, block, channels), F32),
            jax.ShapeDtypeStruct((2 * chunks, LANES), F32),
        ),
        in_specs=[hbm] * 5,
        out_specs=(vmem, vmem, vmem),
        scratch_shapes=[
            pltpu.VMEM((slab, channels), BF16),
            pltpu.VMEM((area, half), BF16),
            pltpu.VMEM((area + 2 * width, channels), BF16),
            pltpu.VMEM((TAPS, channels, half), BF16),
            pltpu.VMEM((channels, area + 2 * width), BF16),
            pltpu.VMEM((3, area, half), BF16),
            pltpu.VMEM((area, half), F32),
            pltpu.VMEM((TAPS, chips, 2 * block, half), F32),
            pltpu.VMEM((TAPS, mine, chips // 2, 2 * block, LANES), BF16),
            pltpu.VMEM((TAPS, mine, chips // 2, 2 * block, LANES), BF16),
            pltpu.VMEM((TAPS, mine, chips // 4, 2 * block, LANES), BF16),
            pltpu.VMEM((TAPS, mine, chips // 4, 2 * block, LANES), BF16),
            pltpu.VMEM((TAPS, mine, middle, 2 * block, LANES), BF16),
            pltpu.VMEM((TAPS, mine, middle, 2 * block, LANES), BF16),
            pltpu.VMEM((TAPS, mine, 2, block, LANES), BF16),
            pltpu.VMEM((TAPS, mine, 2, block, LANES), BF16),
            pltpu.VMEM((TAPS, mine, block, LANES), F32),
            pltpu.VMEM((TAPS, mine, block, LANES), F32),
            pltpu.VMEM((slab, half), BF16),
            pltpu.VMEM((slab, half), BF16),
            pltpu.VMEM((n, 1, LANES), F32),
            pltpu.VMEM((n, 1, LANES), F32),
            pltpu.VMEM((n, 2 * mine, LANES), F32),
            pltpu.VMEM((1, channels), F32),
            pltpu.VMEM((1, channels), F32),
            dma((height,)), dma((5,)), dma((3,)), dma((3,)), dma((2,)), dma((2,)),
            dma((n,)), dma((n,)), dma((n,)), dma((n,)), dma((n,)), dma((n,)),
            lots, lots, lots, lots, dma((TAPS, mine, bits)), dma((TAPS, mine, bits)), dma((TAPS, mine, 2)), dma((TAPS, mine, 2)), lots, lots,
        ],
        compiler_params=pltpu.CompilerParams(
            collective_id=0, has_side_effects=True, vmem_limit_bytes=MAIN * 1024 * 1024
        ),
        name="block_backward",
    )(
        *(
            pltpu.with_memory_space_constraint(x, pltpu.HBM)
            for x in (
                features.reshape(slab, channels), grad_out.reshape(slab, channels), by_tap,
                norm_gain.reshape(1, channels), norm_bias.reshape(1, channels),
            )
        ),
    )
    grad_in, filter_grad, gain_grad, bias_grad = pl.pallas_call(
        hand_over,
        out_shape=(
            jax.ShapeDtypeStruct((slab, channels), BF16),
            jax.ShapeDtypeStruct((TAPS, block, channels), F32),
            jax.ShapeDtypeStruct((1, channels), F32),
            jax.ShapeDtypeStruct((1, channels), F32),
        ),
        in_specs=[vmem, vmem, vmem],
        out_specs=(hbm, hbm, vmem, vmem),
        scratch_shapes=[dma((2,))],
        compiler_params=pltpu.CompilerParams(vmem_limit_bytes=8 * 1024 * 1024),
        name="hand_over",
    )(grad_in, filter_grad, sums)
    return (
        grad_in.reshape(height, width, channels),
        filter_grad.transpose(1, 0, 2).reshape(block, 3, 3, channels),
        gain_grad.reshape(channels),
        bias_grad.reshape(channels),
    )


def solution(mesh):
    slabs = P(("parts", "rows"), None, None)
    return jax.shard_map(
        functools.partial(local, mesh.shape["rows"]),
        mesh=mesh,
        in_specs=(slabs, slabs, P(), P(), P()),
        out_specs=(slabs, P(("parts", "rows"), None, None, None), P("parts"), P("parts")),
        check_vma=False,
    )
```

time: 57.5 us -> 64.2 us (1.12)
  Pallas kernels: 53.6 us -> 63.4 us
  local copies, waits for them, and re-layouts: 2.96 us -> 0 us
    pallas_call x1, Pallas kernels: 51.9 us -> 61.7 us  [local(): pl.pallas_call(functools.partial(kernel, n, height, width, channels), out...]
    unnamed x6 -> x0, local copies, waits for them, and re-layouts: 2.96 us -> none
where the time goes in v1:
time: 64.2 us; the launch traced here: 64.1 us
  Pallas kernels  63.4 us (99%)
    pallas_call x1, Pallas kernels, local(): pl.pallas_call(functools.partial(kernel, n, height, width, channels), out...  61.7 us
    pallas_call x1, Pallas kernels, local(): pl.pallas_call(hand_over, out_shape=(jax.ShapeDtypeStruct((slab, channels...  1.76 us

profile of v1, /device:TPU:0, one launch (start us, length us, event | category | flops | bytes accessed | tf_op | source)
XLA Modules:
  0.0 64.1 jit_solution(6508357833161523240)
XLA Ops:
  0.6 61.7 %block_backward.1 = (bf16[1024,512]{1,0:T(8,128)(2,1)S(1)}, f32[9,32,512]{2,1,0:T(8,128)S(1)}, f32[8,128]{1,0:T(8,128)S(1)}) custom-call(bf16[1024,512]{1,0:T(8,128)(2,1)} %bitcast.14, bf16[1024,512]{1,0:T(8,128)(2,1)} %bitcast.15, bf16[9,512,512]{2,1,0:T(8,128)(2,1)} %bitcast.13, f32[1,512]{1,0:T(1,128)} %bitcast.16, f32[1,512]{1,0:T(1,128)} %bitcast.17), custom_call_target="tpu_custom_call" | custom-call | tf_op jit(solution)/shard_map/block_backward/pallas_call | solution.py:642
  62.3 1.8 %hand_over.1 = (bf16[1024,512]{1,0:T(8,128)(2,1)}, f32[9,32,512]{2,1,0:T(8,128)}, f32[1,512]{1,0:T(1,128)}, f32[1,512]{1,0:T(1,128)}) custom-call(bf16[1024,512]{1,0:T(8,128)(2,1)S(1)} %get-tuple-element.11.gin, f32[9,32,512]{2,1,0:T(8,128)S(1)} %get-tuple-element.12.fg, f32[8,128]{1,0:T(8,128)S(1)} %get-tuple-element.13.sums), custom_call_target="tpu_custom_call" | custom-call | tf_op jit(solution)/shard_map/hand_over/pallas_call | solution.py:694

commit v2 on v1

--- a/solution.py
+++ b/solution.py
@@ -13,6 +13,8 @@
 POWER = 9
 TAPS = 9
 LAG_B = 2
+GAP = 2
+LAST = 2
 MAIN = 40
 EPSILON = 1e-06
 GAIN_MAX = 1.75
@@ -51,11 +53,11 @@
     n, height, width, channels,
     feat_hbm, gout_hbm, filt_hbm, gain_hbm, bias_hbm,
     gin_ref, fg_ref, sums_ref,
-    feat, featc, gext, filt, gt, act, gact, part, sa, ra, sb, rb, sm, rm, sc, rc, hs, hr,
+    feat, featc, gext, filt, gt, act, gact, part, sa, ra, sb, rb, sm, rm, sc, rc, hs, hr, both,
     gin_s, gin_r, stat, tops, sums, gain_ref, bias_ref,
     feat_sem, local_sem, push_send, push_recv, halo_send, halo_recv,
-    stat_send, stat_recv, tops_send, tops_recv, sums_send, sums_recv,
-    a_send, a_recv, b_send, b_recv, m_send, m_recv, c_send, c_recv, h_send, h_recv,
+    share_send, share_recv,
+    out_send, a_recv, b_recv, m_recv, c_recv,
 ):
     me = lax.axis_index("rows")
     core, chip = lax.rem(me, 2), lax.div(me, 2)
@@ -111,10 +113,6 @@
     for copy in in_feat:
         copy.start()
     in_gout.start()
-    in_half.start()
-    in_filt.start()
-    in_gain.start()
-    in_bias.start()
 
     barrier = pltpu.get_barrier_semaphore()
 
@@ -124,33 +122,25 @@
 
     lax.fori_loop(1, n, greet, 0)
 
-    def shared(buffer, send, recv):
-        def copy(k, source):
-            return remote(buffer.at[me], buffer.at[source], send.at[k], recv.at[source], peer(k))
+    def shared(buffer, j):
+        def copy(k):
+            return remote(
+                buffer.at[me], buffer.at[me], share_send.at[j], share_recv.at[j], peer(k)
+            )
 
         def start():
             def body(k, carry):
-                copy(k, me).start()
+                copy(k).start()
                 return carry
             lax.fori_loop(1, n, body, 0)
 
-        def wait():
-            def body(k, carry):
-                copy(k, peer(k)).wait_recv()
-                return carry
-            lax.fori_loop(1, n, body, 0)
-
-        def drain():
-            def body(k, carry):
-                copy(k, me).wait_send()
-                return carry
-            lax.fori_loop(1, n, body, 0)
-
-        return start, wait, drain
-
-    stat_start, stat_wait, stat_drain = shared(stat, stat_send, stat_recv)
-    tops_start, tops_wait, tops_drain = shared(tops, tops_send, tops_recv)
-    sums_start, sums_wait, sums_drain = shared(sums, sums_send, sums_recv)
+        others = buffer.at[pl.ds(0, n - 1)]
+        every = remote(others, others, share_send.at[j], share_recv.at[j], mate)
+        return start, every.wait_recv, every.wait_send
+
+    stat_start, stat_wait, stat_drain = shared(stat, 0)
+    tops_start, tops_wait, tops_drain = shared(tops, 1)
+    sums_start, sums_wait, sums_drain = shared(sums, 2)
 
     lane = lax.broadcasted_iota(jnp.int32, (1, LANES), 1)
     slot = lane & (per_group - 1)
@@ -182,30 +172,14 @@
         gext.at[pl.ds(width + own, slab)], gext.at[pl.ds(width + own, slab)],
         push_send.at[1], push_recv.at[1], mate,
     )
-    push_feat.start()
-    in_gout.wait()
-    push_gout.start()
-
     above, below = pl.ds(0, width), pl.ds((tall + 1) * width, width)
     first, last = pl.ds(width, width), pl.ds(tall * width, width)
 
-    def to_above(k):
-        return remote(gext.at[first], gext.at[below], halo_send.at[k], halo_recv.at[0], me - 1 - k)
-
-    def to_below(k):
-        return remote(gext.at[last], gext.at[above], halo_send.at[k], halo_recv.at[1], me + 1 + k)
-
+    to_above = remote(gext.at[first], gext.at[below], halo_send.at[0], halo_recv.at[0], me - 1)
+    to_below = remote(gext.at[last], gext.at[above], halo_send.at[0], halo_recv.at[0], me + 1)
+    pass_above = remote(gext.at[above], gext.at[above], halo_send.at[1], halo_recv.at[1], mate)
+    pass_below = remote(gext.at[below], gext.at[below], halo_send.at[1], halo_recv.at[1], mate)
     has_above, has_below = chip > 0, chip < chips - 1
-
-    @pl.when((core == 0) & has_above)
-    def _():
-        to_above(0).start()
-        to_above(1).start()
-
-    @pl.when((core == 1) & has_below)
-    def _():
-        to_below(0).start()
-        to_below(1).start()
 
     @pl.when(chip == 0)
     def _():
@@ -214,6 +188,8 @@
     @pl.when(chip == chips - 1)
     def _():
         gext[below, :] = jnp.zeros((width, channels), BF16)
+
+    in_gout.wait()
 
     def top_step(h, carry):
         g = jnp.abs(gext[rows_of(1 + core * height + h), :])
@@ -226,6 +202,21 @@
         top = jnp.maximum(top, largest[:, c * LANES:(c + 1) * LANES])
     tops[me] = top
     tops_start()
+    push_feat.start()
+    push_gout.start()
+
+    @pl.when((core == 0) & has_above)
+    def _():
+        to_above.start()
+
+    @pl.when((core == 1) & has_below)
+    def _():
+        to_below.start()
+
+    in_half.start()
+    in_filt.start()
+    in_gain.start()
+    in_bias.start()
 
     column = lax.broadcasted_iota(jnp.int32, (width, LANES), 0)
 
@@ -236,7 +227,9 @@
         return jnp.where(column < width - 1, pltpu.roll(x, width - 1, 0), 0.0)
 
     def conv(j):
-        first_row = lax.rem(core * height + 1 + 2 * j, tall)
+        turned = core * (height - 2 - 2 * j) + j
+        inner = lax.div(height - 1 - j + tall - 3, tall - 2)
+        first_row = 1 + 2 * (inner * turned + (1 - inner) * j)
         where = [first_row, lax.rem(first_row + 1, tall)]
         ys = [[], []]
         for s in range(3):
@@ -269,8 +262,7 @@
 
     transposes(1 + core * height, height)
     in_filt.wait()
-    if height >= 4:
-        conv(0)
+    conv(0)
 
     push_gout_in = remote(
         gext.at[pl.ds(width + other, slab)], gext.at[pl.ds(width + other, slab)],
@@ -283,19 +275,6 @@
     push_gout_in.wait_recv()
     transposes(1 + (1 - core) * height, height)
 
-    @pl.when(has_below)
-    def _():
-        to_above(0).wait_recv()
-
-    @pl.when(has_above)
-    def _():
-        to_below(0).wait_recv()
-
-    transpose(0)
-    transpose(tall + 1)
-    if height < 4:
-        conv(0)
-    conv(1)
     in_half.wait()
     in_gain.wait()
     in_bias.wait()
@@ -346,8 +325,9 @@
         return carry
 
     def multiply(t):
-        s = lax.rem(1 + 2 * lax.div(t, 3), 3)
-        start = pl.multiple_of((2 - lax.rem(t, 3)) * width, LANES)
+        s = lax.rem(1 + 2 * lax.rem(t, 3), 3)
+        r = lax.rem(1 + 2 * lax.div(t, 3), 3)
+        start = pl.multiple_of((2 - r) * width, LANES)
         for m in range(2):
             result = jnp.dot(
                 gt[m * half:(m + 1) * half, pl.ds(start, area)], act[s],
@@ -365,28 +345,28 @@
 
     def copy_a(t, k):
         target = me + pair_delta(swapped(t, k))
-        return remote(sa.at[t, k], ra.at[t, k], a_send.at[t, k], a_recv.at[t, k], target)
+        return remote(sa.at[t, k], ra.at[t, k], out_send.at[0], a_recv.at[t, k], target)
 
     def copy_b(t, k):
         target = me + pair_delta(1 - swapped(t, k))
-        return remote(sb.at[t, k], rb.at[t, k], b_send.at[t, k], b_recv.at[t, k], target)
+        return remote(sb.at[t, k], rb.at[t, k], out_send.at[1], b_recv.at[t, k], target)
 
     def copy_m(t, k, j):
         at = pl.ds(chips // 4 - (chips >> j), chips >> (j + 1))
         return remote(
             sm.at[t, k, at], rm.at[t, k, at],
-            m_send.at[t, k, j], m_recv.at[t, k, j], me + across[j],
+            out_send.at[2], m_recv.at[t, k, j - 2], me + across[j],
         )
 
     def copy_c(t, k, way, source):
         target = lax.div(me + across[bits - 1], 2) * 2 + way
         return remote(
             sc.at[t, k, way], rc.at[t, k, source],
-            c_send.at[t, k, way], c_recv.at[t, k, source], target,
+            out_send.at[3], c_recv.at[t, k], target,
         )
 
     def copy_h(t, k):
-        return remote(hs.at[t, k], hr.at[t, k], h_send.at[t, k], h_recv.at[t, k], mate)
+        return remote(hs.at[t, k], hr.at[t, k], out_send.at[4], c_recv.at[t, k], mate)
 
     def lanes_of(k):
         return slice(k * LANES, (k + 1) * LANES)
@@ -455,15 +435,13 @@
         part[t, chip, rows, lanes_of(k)] = value(bit[j], rows)
 
     def stage_d(t, k):
-        tap = 3 * lax.rem(t, 3) + lax.rem(1 + 2 * lax.div(t, 3), 3)
+        tap = 3 * lax.rem(1 + 2 * lax.div(t, 3), 3) + lax.rem(1 + 2 * lax.rem(t, 3), 3)
         rows = pl.ds(pl.multiple_of(core * block, block), block)
-        copy_c(t, k, core, core).wait_recv()
+        remote(both, both, out_send.at[3], c_recv.at[t, k], mate).wait_recv()
         total = part[t, chip, rows, lanes_of(k)]
         total = total + decode(rc[t, k, core])
         at = pl.ds(pl.multiple_of(my_cols + k * LANES, LANES), LANES)
         fg_ref[tap, :, at] = total * (reach / pixels)
-        copy_h(t, k).wait_recv()
-        copy_c(t, k, core, 1 - core).wait_recv()
         total = hr[t, k] + decode(rc[t, k, 1 - core])
         at = pl.ds(pl.multiple_of(mate_cols + k * LANES, LANES), LANES)
         fg_ref[tap, :, at] = total * (reach / pixels)
@@ -526,7 +504,8 @@
             if side:
                 push_gin.start()
 
-    lag_d = LAG_B + bits - 1
+    lag_c = LAG_B + GAP * (bits - 2)
+    lag_d = lag_c + LAST
 
     def run(t, carry):
         @pl.when(t < TAPS)
@@ -539,15 +518,38 @@
         def _():
             lax.fori_loop(0, tall, shift, 0)
 
-        @pl.when((t >= 1) & (t < height - 1))
-        def _():
-            conv(t + 1)
-
-        @pl.when(t == 3)
+            @pl.when((core == 0) & has_above)
+            def _():
+                to_below.wait_recv()
+                pass_above.start()
+
+            @pl.when((core == 1) & has_below)
+            def _():
+                to_above.wait_recv()
+                pass_below.start()
+
+        @pl.when(t == 2)
+        def _():
+            @pl.when((core == 1) & has_above)
+            def _():
+                pass_above.wait_recv()
+
+            @pl.when((core == 0) & has_below)
+            def _():
+                pass_below.wait_recv()
+
+            transpose(0)
+            transpose(tall + 1)
+
+        @pl.when((t >= 1) & (t < height))
+        def _():
+            conv(t)
+
+        @pl.when(t == height)
         def _():
             gradients()
 
-        @pl.when(t == 6)
+        @pl.when(t == 10)
         def _():
             finish()
 
@@ -557,15 +559,17 @@
                 stage_b(t - LAG_B, k)
 
         for j in range(2, bits - 1):
-            @pl.when((t >= LAG_B + j - 1) & (t < TAPS + LAG_B + j - 1))
+            lag_m = LAG_B + GAP * (j - 1)
+
+            @pl.when((t >= lag_m) & (t < TAPS + lag_m))
             def _():
                 for k in range(mine):
-                    stage_m(t - LAG_B - j + 1, k, j)
-
-        @pl.when((t >= lag_d - 1) & (t < TAPS + lag_d - 1))
+                    stage_m(t - lag_m, k, j)
+
+        @pl.when((t >= lag_c) & (t < TAPS + lag_c))
         def _():
             for k in range(mine):
-                stage_c(t - lag_d + 1, k)
+                stage_c(t - lag_c, k)
 
         @pl.when(t >= lag_d)
         def _():
@@ -584,18 +588,9 @@
 
     lax.fori_loop(0, height, collect, 0)
 
-    def drain(t, carry):
-        for k in range(mine):
-            copy_a(t, k).wait_send()
-            copy_b(t, k).wait_send()
-            for j in range(2, bits - 1):
-                copy_m(t, k, j).wait_send()
-            for way in range(2):
-                copy_c(t, k, way, core).wait_send()
-            copy_h(t, k).wait_send()
-        return carry
-
-    lax.fori_loop(0, TAPS, drain, 0)
+    for j, (source, target) in enumerate(((sa, ra), (sb, rb), (sm, rm), (sc, rc), (hs, hr))):
+        if j != 2 or bits > 3:
+            remote(source, target, out_send.at[j], out_send.at[j], mate).wait_send()
     push_feat.wait_send()
     push_gout.wait_send()
     push_gin.wait_send()
@@ -605,13 +600,13 @@
 
     @pl.when((core == 0) & has_above)
     def _():
-        to_above(0).wait_send()
-        to_above(1).wait_send()
+        to_above.wait_send()
+        pass_above.wait_send()
 
     @pl.when((core == 1) & has_below)
     def _():
-        to_below(0).wait_send()
-        to_below(1).wait_send()
+        to_below.wait_send()
+        pass_below.wait_send()
 
 
 def hand_over(gin, fg, sums, gin_out, fg_out, gain_out, bias_out, sem):
@@ -667,6 +662,7 @@
             pltpu.VMEM((TAPS, mine, 2, block, LANES), BF16),
             pltpu.VMEM((TAPS, mine, block, LANES), F32),
             pltpu.VMEM((TAPS, mine, block, LANES), F32),
+            pltpu.VMEM((2, block, LANES), F32),
             pltpu.VMEM((slab, half), BF16),
             pltpu.VMEM((slab, half), BF16),
             pltpu.VMEM((n, 1, LANES), F32),
@@ -675,8 +671,8 @@
             pltpu.VMEM((1, channels), F32),
             pltpu.VMEM((1, channels), F32),
             dma((height,)), dma((5,)), dma((3,)), dma((3,)), dma((2,)), dma((2,)),
-            dma((n,)), dma((n,)), dma((n,)), dma((n,)), dma((n,)), dma((n,)),
-            lots, lots, lots, lots, dma((TAPS, mine, bits)), dma((TAPS, mine, bits)), dma((TAPS, mine, 2)), dma((TAPS, mine, 2)), lots, lots,
+            dma((3,)), dma((3,)),
+            dma((5,)), lots, lots, dma((TAPS, mine, middle)), lots,
         ],
         compiler_params=pltpu.CompilerParams(
             collective_id=0, has_side_effects=True, vmem_limit_bytes=MAIN * 1024 * 1024

time: 64.2 us -> 47.2 us (0.74)
  Pallas kernels: 63.4 us -> 46.4 us
    pallas_call x1, Pallas kernels: 61.7 us -> 44.6 us  [local(): pl.pallas_call(functools.partial(kernel, n, height, width, channels), out...]
where the time goes in v2:
time: 47.2 us; the launch traced here: 47 us
  Pallas kernels  46.4 us (98%)
  between operations  0.64 us (1%)
    pallas_call x1, Pallas kernels, local(): pl.pallas_call(functools.partial(kernel, n, height, width, channels), out...  44.6 us
    pallas_call x1, Pallas kernels, local(): pl.pallas_call(hand_over, out_shape=(jax.ShapeDtypeStruct((slab, channels...  1.76 us

profile of v2, /device:TPU:0, one launch (start us, length us, event | category | flops | bytes accessed | tf_op | source)
XLA Modules:
  0.0 47.0 jit_solution(662540345163767921)
XLA Ops:
  0.6 44.6 %block_backward.1 = (bf16[1024,512]{1,0:T(8,128)(2,1)S(1)}, f32[9,32,512]{2,1,0:T(8,128)S(1)}, f32[8,128]{1,0:T(8,128)S(1)}) custom-call(bf16[1024,512]{1,0:T(8,128)(2,1)} %bitcast.14, bf16[1024,512]{1,0:T(8,128)(2,1)} %bitcast.15, bf16[9,512,512]{2,1,0:T(8,128)(2,1)} %bitcast.13, f32[1,512]{1,0:T(1,128)} %bitcast.16, f32[1,512]{1,0:T(1,128)} %bitcast.17), custom_call_target="tpu_custom_call" | custom-call | tf_op jit(solution)/shard_map/block_backward/pallas_call | solution.py:637
  45.3 1.8 %hand_over.1 = (bf16[1024,512]{1,0:T(8,128)(2,1)}, f32[9,32,512]{2,1,0:T(8,128)}, f32[1,512]{1,0:T(1,128)}, f32[1,512]{1,0:T(1,128)}) custom-call(bf16[1024,512]{1,0:T(8,128)(2,1)S(1)} %get-tuple-element.11.gin, f32[9,32,512]{2,1,0:T(8,128)S(1)} %get-tuple-element.12.fg, f32[8,128]{1,0:T(8,128)S(1)} %get-tuple-element.13.sums), custom_call_target="tpu_custom_call" | custom-call | tf_op jit(solution)/shard_map/hand_over/pallas_call | solution.py:690

commit v3 on v2

--- a/solution.py
+++ b/solution.py
@@ -12,9 +12,17 @@
 LANES = 128
 POWER = 9
 TAPS = 9
-LAG_B = 2
-GAP = 2
-LAST = 2
+SWAPPED = 5
+PLAN = (
+    ("shift", "relay"), (), ("conv1", "edges"), ("b00",), ("b10",), ("b01", "conv2", "b20"),
+    ("b30", "c00", "conv3", "b40", "c10"), ("grad", "b11", "b50", "c20", "b51"),
+    ("b21", "b31", "b41", "c30", "c01", "c40"),
+)
+REST = (
+    "b60", "b61", "c50", "c51", "b70", "c60", "d00", "b71", "c11", "c61", "d10", "d20",
+    "b80", "c70", "fin1", "b81", "c71", "c21", "c31", "c80", "c41", "d30", "c81", "fin0", "d40",
+    "d01", "d50", "d51", "d60", "d11", "d61", "d70", "d71", "d21", "d31", "d80", "d41", "d81",
+)
 MAIN = 40
 EPSILON = 1e-06
 GAIN_MAX = 1.75
@@ -112,7 +120,6 @@
     in_bias = pltpu.make_async_copy(bias_hbm, bias_ref, local_sem.at[4])
     for copy in in_feat:
         copy.start()
-    in_gout.start()
 
     barrier = pltpu.get_barrier_semaphore()
 
@@ -121,6 +128,8 @@
         return carry
 
     lax.fori_loop(1, n, greet, 0)
+
+    in_gout.start()
 
     def shared(buffer, j):
         def copy(k):
@@ -153,6 +162,10 @@
             x = x.reshape(width // 8, 8, LANES)
             totals[c] = totals[c] + x.sum(0)
             squares[c] = squares[c] + (x * x).sum(0)
+    in_half.start()
+    in_filt.start()
+    in_gain.start()
+    in_bias.start()
     packed = jnp.zeros((1, LANES), F32)
     for c in range(chunks):
         total = group_sum(totals[c].sum(0, keepdims=True), per_group)
@@ -161,34 +174,6 @@
         packed = packed + jnp.where(slot == chunks + c, square, 0.0)
     stat[me] = packed
 
-    pl.semaphore_wait(barrier, n - 1)
-    stat_start()
-
-    push_feat = remote(
-        feat.at[:, pl.ds(mate_cols, half)], featc.at[pl.ds(own, slab)],
-        push_send.at[0], push_recv.at[0], mate,
-    )
-    push_gout = remote(
-        gext.at[pl.ds(width + own, slab)], gext.at[pl.ds(width + own, slab)],
-        push_send.at[1], push_recv.at[1], mate,
-    )
-    above, below = pl.ds(0, width), pl.ds((tall + 1) * width, width)
-    first, last = pl.ds(width, width), pl.ds(tall * width, width)
-
-    to_above = remote(gext.at[first], gext.at[below], halo_send.at[0], halo_recv.at[0], me - 1)
-    to_below = remote(gext.at[last], gext.at[above], halo_send.at[0], halo_recv.at[0], me + 1)
-    pass_above = remote(gext.at[above], gext.at[above], halo_send.at[1], halo_recv.at[1], mate)
-    pass_below = remote(gext.at[below], gext.at[below], halo_send.at[1], halo_recv.at[1], mate)
-    has_above, has_below = chip > 0, chip < chips - 1
-
-    @pl.when(chip == 0)
-    def _():
-        gext[above, :] = jnp.zeros((width, channels), BF16)
-
-    @pl.when(chip == chips - 1)
-    def _():
-        gext[below, :] = jnp.zeros((width, channels), BF16)
-
     in_gout.wait()
 
     def top_step(h, carry):
@@ -201,9 +186,37 @@
     for c in range(chunks):
         top = jnp.maximum(top, largest[:, c * LANES:(c + 1) * LANES])
     tops[me] = top
+    push_feat = remote(
+        feat.at[:, pl.ds(mate_cols, half)], featc.at[pl.ds(own, slab)],
+        push_send.at[0], push_recv.at[0], mate,
+    )
+    push_gout = remote(
+        gext.at[pl.ds(width + own, slab)], gext.at[pl.ds(width + own, slab)],
+        push_send.at[1], push_recv.at[1], mate,
+    )
+    pl.semaphore_wait(barrier, n - 1)
+    stat_start()
     tops_start()
+    push_gout.start()
     push_feat.start()
-    push_gout.start()
+
+    above, below = pl.ds(0, width), pl.ds((tall + 1) * width, width)
+    first, last = pl.ds(width, width), pl.ds(tall * width, width)
+
+    to_above = remote(gext.at[first], gext.at[below], halo_send.at[0], halo_recv.at[0], me - 1)
+    to_below = remote(gext.at[last], gext.at[above], halo_send.at[0], halo_recv.at[0], me + 1)
+    pass_above = remote(gext.at[above], gext.at[above], halo_send.at[1], halo_recv.at[1], mate)
+    pass_below = remote(gext.at[below], gext.at[below], halo_send.at[1], halo_recv.at[1], mate)
+    has_above, has_below = chip > 0, chip < chips - 1
+
+    @pl.when(chip == 0)
+    def _():
+        gext[above, :] = jnp.zeros((width, channels), BF16)
+
+    @pl.when(chip == chips - 1)
+    def _():
+        gext[below, :] = jnp.zeros((width, channels), BF16)
+
 
     @pl.when((core == 0) & has_above)
     def _():
@@ -213,10 +226,6 @@
     def _():
         to_below.start()
 
-    in_half.start()
-    in_filt.start()
-    in_gain.start()
-    in_bias.start()
 
     column = lax.broadcasted_iota(jnp.int32, (width, LANES), 0)
 
@@ -337,8 +346,11 @@
                 chips // 2, 2 * block, half
             )
 
+    def reached(t, least):
+        return lax.div(t + TAPS - least, TAPS)
+
     def swapped(t, k):
-        return (1 - lax.rem(t, 2)) * k
+        return k * (1 - reached(t, SWAPPED))
 
     def pair_delta(kind):
         return kind * across[1] + (1 - kind) * across[0]
@@ -478,107 +490,94 @@
                 sums_ref[chunks + c * mine + k:chunks + c * mine + k + 1, :] = (
                     everyone[c, mine + k:mine + k + 1]
                 )
-        for side in (1, 0):
-            base = (1 - core if side else core) * height
-            for k in range(mine):
-                mean_grad = group_sum(
-                    gains[k] * sums_ref[pl.ds(core * mine + k, 1), :], per_group
-                ) / members
-                mean_cross = group_sum(
-                    gains[k] * sums_ref[pl.ds(chunks + core * mine + k, 1), :], per_group
-                ) / members
-                at = pl.ds(pl.multiple_of(my_cols + k * LANES, LANES), LANES)
-
-                def final_step(h, carry):
-                    rows = rows_of(base + h)
-                    cols = lanes_of(k)
-                    normalized = (featc[rows, cols].astype(F32) - means[k]) * invs[k]
-                    result = invs[k] * (gact[rows, cols] * gains[k] - mean_grad - normalized * mean_cross)
-                    if side:
-                        gin_s[rows_of(h), cols] = result.astype(BF16)
-                    else:
-                        gin_ref[rows_of(h), at] = result.astype(BF16)
-                    return carry
-
-                lax.fori_loop(0, height, final_step, 0)
-            if side:
-                push_gin.start()
-
-    lag_c = LAG_B + GAP * (bits - 2)
-    lag_d = lag_c + LAST
+        half_finish(1)
+        push_gin.start()
+
+    def half_finish(side):
+        base = (1 - core if side else core) * height
+        for k in range(mine):
+            mean_grad = group_sum(
+                gains[k] * sums_ref[pl.ds(core * mine + k, 1), :], per_group
+            ) / members
+            mean_cross = group_sum(
+                gains[k] * sums_ref[pl.ds(chunks + core * mine + k, 1), :], per_group
+            ) / members
+            at = pl.ds(pl.multiple_of(my_cols + k * LANES, LANES), LANES)
+
+            def final_step(h, carry):
+                rows = rows_of(base + h)
+                cols = lanes_of(k)
+                normalized = (featc[rows, cols].astype(F32) - means[k]) * invs[k]
+                result = invs[k] * (gact[rows, cols] * gains[k] - mean_grad - normalized * mean_cross)
+                if side:
+                    gin_s[rows_of(h), cols] = result.astype(BF16)
+                else:
+                    gin_ref[rows_of(h), at] = result.astype(BF16)
+                return carry
+
+            lax.fori_loop(0, height, final_step, 0)
+
+    def relay():
+        @pl.when((core == 0) & has_above)
+        def _():
+            to_below.wait_recv()
+            pass_above.start()
+
+        @pl.when((core == 1) & has_below)
+        def _():
+            to_above.wait_recv()
+            pass_below.start()
+
+    def edges():
+        @pl.when((core == 1) & has_above)
+        def _():
+            pass_above.wait_recv()
+
+        @pl.when((core == 0) & has_below)
+        def _():
+            pass_below.wait_recv()
+
+        transpose(0)
+        transpose(tall + 1)
+
+    def shifts():
+        lax.fori_loop(0, tall, shift, 0)
+
+    named = {"shift": shifts, "relay": relay, "edges": edges, "grad": gradients, "fin1": finish,
+        "fin0": functools.partial(half_finish, 0),
+    }
+
+    def perform(name):
+        if name in named:
+            return named[name]()
+        if name.startswith("conv"):
+            j = int(name[4:])
+            return conv(j) if j < height else None
+        t, k = int(name[1]), int(name[2])
+        if name[0] == "b":
+            stage_b(t, k)
+        elif name[0] == "c":
+            for j in range(2, bits - 1):
+                stage_m(t, k, j)
+            stage_c(t, k)
+        else:
+            stage_d(t, k)
 
     def run(t, carry):
-        @pl.when(t < TAPS)
-        def _():
-            multiply(t)
-            for k in range(mine):
-                stage_a(t, k)
-
-        @pl.when(t == 0)
-        def _():
-            lax.fori_loop(0, tall, shift, 0)
-
-            @pl.when((core == 0) & has_above)
-            def _():
-                to_below.wait_recv()
-                pass_above.start()
-
-            @pl.when((core == 1) & has_below)
-            def _():
-                to_above.wait_recv()
-                pass_below.start()
-
-        @pl.when(t == 2)
-        def _():
-            @pl.when((core == 1) & has_above)
-            def _():
-                pass_above.wait_recv()
-
-            @pl.when((core == 0) & has_below)
-            def _():
-                pass_below.wait_recv()
-
-            transpose(0)
-            transpose(tall + 1)
-
-        @pl.when((t >= 1) & (t < height))
-        def _():
-            conv(t)
-
-        @pl.when(t == height)
-        def _():
-            gradients()
-
-        @pl.when(t == 10)
-        def _():
-            finish()
-
-        @pl.when((t >= LAG_B) & (t < TAPS + LAG_B))
-        def _():
-            for k in range(mine):
-                stage_b(t - LAG_B, k)
-
-        for j in range(2, bits - 1):
-            lag_m = LAG_B + GAP * (j - 1)
-
-            @pl.when((t >= lag_m) & (t < TAPS + lag_m))
-            def _():
-                for k in range(mine):
-                    stage_m(t - lag_m, k, j)
-
-        @pl.when((t >= lag_c) & (t < TAPS + lag_c))
-        def _():
-            for k in range(mine):
-                stage_c(t - lag_c, k)
-
-        @pl.when(t >= lag_d)
-        def _():
-            for k in range(mine):
-                stage_d(t - lag_d, k)
-
+        multiply(t)
+        for k in range(mine):
+            stage_a(t, k)
+        for step, names in enumerate(PLAN):
+            if names:
+                @pl.when(t == step)
+                def _():
+                    for name in names:
+                        perform(name)
         return carry
 
-    lax.fori_loop(0, TAPS + lag_d, run, 0)
+    lax.fori_loop(0, TAPS, run, 0)
+    for name in REST:
+        perform(name)
 
     push_gin.wait_recv()
 
@@ -610,17 +609,19 @@
 
 
 def hand_over(gin, fg, sums, gin_out, fg_out, gain_out, bias_out, sem):
-    first = pltpu.make_async_copy(gin, gin_out, sem.at[0])
-    second = pltpu.make_async_copy(fg, fg_out, sem.at[1])
-    first.start()
-    second.start()
+    copies = (
+        pltpu.make_async_copy(gin, gin_out, sem.at[0]),
+        pltpu.make_async_copy(fg, fg_out, sem.at[1]),
+    )
+    for copy in copies:
+        copy.start()
     chunks = sums.shape[0] // 2
     for c in range(chunks):
         cols = slice(c * LANES, (c + 1) * LANES)
         bias_out[:, cols] = sums[c:c + 1, :]
         gain_out[:, cols] = sums[chunks + c:chunks + c + 1, :]
-    first.wait()
-    second.wait()
+    for copy in copies:
+        copy.wait()
 
 
 def local(n, features, grad_out, filters, norm_gain, norm_bias):
@@ -672,7 +673,7 @@
             pltpu.VMEM((1, channels), F32),
             dma((height,)), dma((5,)), dma((3,)), dma((3,)), dma((2,)), dma((2,)),
             dma((3,)), dma((3,)),
-            dma((5,)), lots, lots, dma((TAPS, mine, middle)), lots,
+            dma((5,)), lots, lots, dma((TAPS, mine, bits - 3) if bits > 3 else (1,)), lots,
         ],
         compiler_params=pltpu.CompilerParams(
             collective_id=0, has_side_effects=True, vmem_limit_bytes=MAIN * 1024 * 1024

time: 47.2 us -> 44.9 us (0.951)
  Pallas kernels: 46.4 us -> 44.1 us
    pallas_call x1, Pallas kernels: 44.6 us -> 42.4 us  [local(): pl.pallas_call(functools.partial(kernel, n, height, width, channels), out...]
where the time goes in v3:
time: 44.9 us; the launch traced here: 44.8 us
  Pallas kernels  44.1 us (98%)
  between operations  0.64 us (1%)
    pallas_call x1, Pallas kernels, local(): pl.pallas_call(functools.partial(kernel, n, height, width, channels), out...  42.4 us
    pallas_call x1, Pallas kernels, local(): pl.pallas_call(hand_over, out_shape=(jax.ShapeDtypeStruct((slab, channels...  1.76 us

profile of v3, /device:TPU:0, one launch (start us, length us, event | category | flops | bytes accessed | tf_op | source)
XLA Modules:
  0.0 44.8 jit_solution(16615749218754358631)
XLA Ops:
  0.6 42.4 %block_backward.1 = (bf16[1024,512]{1,0:T(8,128)(2,1)S(1)}, f32[9,32,512]{2,1,0:T(8,128)S(1)}, f32[8,128]{1,0:T(8,128)S(1)}) custom-call(bf16[1024,512]{1,0:T(8,128)(2,1)} %bitcast.14, bf16[1024,512]{1,0:T(8,128)(2,1)} %bitcast.15, bf16[9,512,512]{2,1,0:T(8,128)(2,1)} %bitcast.13, f32[1,512]{1,0:T(1,128)} %bitcast.16, f32[1,512]{1,0:T(1,128)} %bitcast.17), custom_call_target="tpu_custom_call" | custom-call | tf_op jit(solution)/shard_map/block_backward/pallas_call | solution.py:638
  43.0 1.8 %hand_over.1 = (bf16[1024,512]{1,0:T(8,128)(2,1)}, f32[9,32,512]{2,1,0:T(8,128)}, f32[1,512]{1,0:T(1,128)}, f32[1,512]{1,0:T(1,128)}) custom-call(bf16[1024,512]{1,0:T(8,128)(2,1)S(1)} %get-tuple-element.11.gin, f32[9,32,512]{2,1,0:T(8,128)S(1)} %get-tuple-element.12.fg, f32[8,128]{1,0:T(8,128)S(1)} %get-tuple-element.13.sums), custom_call_target="tpu_custom_call" | custom-call | tf_op jit(solution)/shard_map/hand_over/pallas_call | solution.py:691

commit v4 on v3

--- a/solution.py
+++ b/solution.py
@@ -13,16 +13,9 @@
 POWER = 9
 TAPS = 9
 SWAPPED = 5
-PLAN = (
-    ("shift", "relay"), (), ("conv1", "edges"), ("b00",), ("b10",), ("b01", "conv2", "b20"),
-    ("b30", "c00", "conv3", "b40", "c10"), ("grad", "b11", "b50", "c20", "b51"),
-    ("b21", "b31", "b41", "c30", "c01", "c40"),
-)
-REST = (
-    "b60", "b61", "c50", "c51", "b70", "c60", "d00", "b71", "c11", "c61", "d10", "d20",
-    "b80", "c70", "fin1", "b81", "c71", "c21", "c31", "c80", "c41", "d30", "c81", "fin0", "d40",
-    "d01", "d50", "d51", "d60", "d11", "d61", "d70", "d71", "d21", "d31", "d80", "d41", "d81",
-)
+TURNED = 2
+PLAN = (("shift", ), (), ("relay_b", "conv1", "edge_b", ), ("b00", "b01", ), ("b10", "b11", "relay_a", ), ("conv2", "b20", "edge_a", ), ("b30", "conv3", "b40", "c00", ), ("grad", "b50", "c10", "b51", ), ("b21", "b31", "b41", "c01", "c11", "b60", "c20", "c30", ))
+REST = ("b61", "c40", "b70", "c50", "b71", "c51", "c60", "b80", "c61", "d00", "d10", "b81", "c70", "d20", "d30", "c21", "fin1", "c71", "c31", "c41", "fin0", "c80", "c81", "d40", "d50", "d51", "d60", "d61", "d01", "d11", "d70", "d21", "d71", "d31", "d41", "d80", "d81", )
 MAIN = 40
 EPSILON = 1e-06
 GAIN_MAX = 1.75
@@ -352,26 +345,29 @@
     def swapped(t, k):
         return k * (1 - reached(t, SWAPPED))
 
-    def pair_delta(kind):
-        return kind * across[1] + (1 - kind) * across[0]
+    def order_of(t, k):
+        if k == 0 or t >= SWAPPED:
+            return list(range(bits))
+        return [1, 2, 0] + list(range(3, bits)) if t < TURNED else [1, 0] + list(range(2, bits))
 
     def copy_a(t, k):
-        target = me + pair_delta(swapped(t, k))
+        kind = swapped(t, k)
+        target = me + kind * across[1] + (1 - kind) * across[0]
         return remote(sa.at[t, k], ra.at[t, k], out_send.at[0], a_recv.at[t, k], target)
 
     def copy_b(t, k):
-        target = me + pair_delta(1 - swapped(t, k))
+        target = me + across[order_of(t, k)[1]]
         return remote(sb.at[t, k], rb.at[t, k], out_send.at[1], b_recv.at[t, k], target)
 
     def copy_m(t, k, j):
         at = pl.ds(chips // 4 - (chips >> j), chips >> (j + 1))
         return remote(
             sm.at[t, k, at], rm.at[t, k, at],
-            out_send.at[2], m_recv.at[t, k, j - 2], me + across[j],
+            out_send.at[2], m_recv.at[t, k, j - 2], me + across[order_of(t, k)[j]],
         )
 
     def copy_c(t, k, way, source):
-        target = lax.div(me + across[bits - 1], 2) * 2 + way
+        target = lax.div(me + across[order_of(t, k)[-1]], 2) * 2 + way
         return remote(
             sc.at[t, k, way], rc.at[t, k, source],
             out_send.at[3], c_recv.at[t, k], target,
@@ -391,60 +387,51 @@
             sa[t, k, w] = encode(part[t, dest, :, lanes_of(k)] * scale)
         copy_a(t, k).start()
 
-    def stage_b(t, k):
-        copy_a(t, k).wait_recv()
-        kind = swapped(t, k)
-        mine_bit = kind * bit[0] + (1 - kind) * bit[1]
-
-        def value(u, v):
-            dest = u * 4 + kind * (2 * bit[1] + v) + (1 - kind) * (2 * v + bit[0])
-            return part[t, dest, :, lanes_of(k)] * scale + decode(ra[t, k, 2 * u + v])
-
-        for u in range(chips // 4):
-            sb[t, k, u] = encode(value(u, 1 - mine_bit))
-        copy_b(t, k).start()
-        for u in range(chips // 4):
-            part[t, u * 4 + 2 * bit[1] + bit[0], :, lanes_of(k)] = value(u, mine_bit)
-
-    def low(j):
-        return lax.rem(chip, 1 << j)
-
-    def received(t, k, j):
-        if j == 2:
+    def hop(t, k, i):
+        order = order_of(t, k)
+        before = sorted(set(range(bits)) - set(order[:i]))
+        rest = [b for b in before if b != order[i]]
+        here = bit[order[i]]
+        if i == 1:
+            copy_a(t, k).wait_recv()
+            buffer, base = ra, 0
+        elif i == 2:
             copy_b(t, k).wait_recv()
-            return rb, 0
-        copy_m(t, k, j - 1).wait_recv()
-        return rm, chips // 4 - (chips >> (j - 1))
-
-    def stage_m(t, k, j):
-        buffer, base = received(t, k, j)
-
-        def value(r, side):
-            coded = buffer[t, k, base + 2 * r + side]
-            return part[t, (2 * r + side) * (1 << j) + low(j), :, lanes_of(k)] + decode(coded)
-
-        for r in range(chips >> (j + 1)):
-            sm[t, k, chips // 4 - (chips >> j) + r] = encode(value(r, 1 - bit[j]))
-        copy_m(t, k, j).start()
-        for r in range(chips >> (j + 1)):
-            part[t, (2 * r + bit[j]) * (1 << j) + low(j), :, lanes_of(k)] = value(r, bit[j])
-
-    def stage_c(t, k):
-        j = bits - 1
-        buffer, base = received(t, k, j)
-
-        def value(side, rows):
-            coded = buffer[t, k, base + side, rows]
-            return part[t, side * (1 << j) + low(j), rows, lanes_of(k)] + decode(coded)
-
+            buffer, base = rb, 0
+        else:
+            copy_m(t, k, i - 1).wait_recv()
+            buffer, base = rm, chips // 4 - (chips >> (i - 1))
+
+        def place(w, side):
+            spot = side * (1 << order[i])
+            for b in order[:i]:
+                spot = spot + bit[b] * (1 << b)
+            return spot + sum(((w >> j) & 1) << b for j, b in enumerate(rest))
+
+        def value(w, side, rows):
+            index = base + side * (1 << before.index(order[i]))
+            index = index + sum(((w >> j) & 1) << before.index(b) for j, b in enumerate(rest))
+            kept = part[t, place(w, side), rows, lanes_of(k)]
+            kept = kept * scale if i == 1 else kept
+            return kept + decode(buffer[t, k, index, rows])
+
+        if i < bits - 1:
+            out = sb if i == 1 else sm
+            first_slot = 0 if i == 1 else chips // 4 - (chips >> i)
+            for w in range(chips >> (i + 1)):
+                out[t, k, first_slot + w] = encode(value(w, 1 - here, slice(None)))
+            (copy_b(t, k) if i == 1 else copy_m(t, k, i)).start()
+            for w in range(chips >> (i + 1)):
+                part[t, place(w, here), :, lanes_of(k)] = value(w, here, slice(None))
+            return
         for way in range(2):
             rows = slice(way * block, (way + 1) * block)
-            sc[t, k, way] = encode(value(1 - bit[j], rows))
+            sc[t, k, way] = encode(value(0, 1 - here, rows))
             copy_c(t, k, way, core).start()
-        hs[t, k] = value(bit[j], pl.ds(pl.multiple_of((1 - core) * block, block), block))
+        hs[t, k] = value(0, here, pl.ds(pl.multiple_of((1 - core) * block, block), block))
         copy_h(t, k).start()
         rows = pl.ds(pl.multiple_of(core * block, block), block)
-        part[t, chip, rows, lanes_of(k)] = value(bit[j], rows)
+        part[t, chip, rows, lanes_of(k)] = value(0, here, rows)
 
     def stage_d(t, k):
         tap = 3 * lax.rem(1 + 2 * lax.div(t, 3), 3) + lax.rem(1 + 2 * lax.rem(t, 3), 3)
@@ -517,33 +504,37 @@
 
             lax.fori_loop(0, height, final_step, 0)
 
-    def relay():
+    def relay_below():
+        @pl.when((core == 1) & has_below)
+        def _():
+            to_above.wait_recv()
+            pass_below.start()
+
+    def relay_above():
         @pl.when((core == 0) & has_above)
         def _():
             to_below.wait_recv()
             pass_above.start()
 
-        @pl.when((core == 1) & has_below)
+    def edge_below():
+        @pl.when((core == 0) & has_below)
         def _():
-            to_above.wait_recv()
-            pass_below.start()
-
-    def edges():
+            pass_below.wait_recv()
+
+        transpose(tall + 1)
+
+    def edge_above():
         @pl.when((core == 1) & has_above)
         def _():
             pass_above.wait_recv()
 
-        @pl.when((core == 0) & has_below)
-        def _():
-            pass_below.wait_recv()
-
         transpose(0)
-        transpose(tall + 1)
 
     def shifts():
         lax.fori_loop(0, tall, shift, 0)
 
-    named = {"shift": shifts, "relay": relay, "edges": edges, "grad": gradients, "fin1": finish,
+    named = {"shift": shifts, "relay_b": relay_below, "relay_a": relay_above,
+        "edge_b": edge_below, "edge_a": edge_above, "grad": gradients, "fin1": finish,
         "fin0": functools.partial(half_finish, 0),
     }
 
@@ -555,11 +546,10 @@
             return conv(j) if j < height else None
         t, k = int(name[1]), int(name[2])
         if name[0] == "b":
-            stage_b(t, k)
+            hop(t, k, 1)
         elif name[0] == "c":
-            for j in range(2, bits - 1):
-                stage_m(t, k, j)
-            stage_c(t, k)
+            for i in range(2, bits):
+                hop(t, k, i)
         else:
             stage_d(t, k)
 

time: 44.9 us -> 43.9 us (0.978)
  Pallas kernels: 44.1 us -> 43.1 us
    pallas_call x1, Pallas kernels: 42.4 us -> 41.3 us  [local(): pl.pallas_call(functools.partial(kernel, n, height, width, channels), out...]
where the time goes in v4:
time: 43.9 us; the launch traced here: 43.7 us
  Pallas kernels  43.1 us (98%)
  between operations  0.64 us (1%)
    pallas_call x1, Pallas kernels, local(): pl.pallas_call(functools.partial(kernel, n, height, width, channels), out...  41.3 us
    pallas_call x1, Pallas kernels, local(): pl.pallas_call(hand_over, out_shape=(jax.ShapeDtypeStruct((slab, channels...  1.76 us

profile of v4, /device:TPU:0, one launch (start us, length us, event | category | flops | bytes accessed | tf_op | source)
XLA Modules:
  0.0 43.7 jit_solution(16945357916144038308)
XLA Ops:
  0.6 41.3 %block_backward.1 = (bf16[1024,512]{1,0:T(8,128)(2,1)S(1)}, f32[9,32,512]{2,1,0:T(8,128)S(1)}, f32[8,128]{1,0:T(8,128)S(1)}) custom-call(bf16[1024,512]{1,0:T(8,128)(2,1)} %bitcast.14, bf16[1024,512]{1,0:T(8,128)(2,1)} %bitcast.15, bf16[9,512,512]{2,1,0:T(8,128)(2,1)} %bitcast.13, f32[1,512]{1,0:T(1,128)} %bitcast.16, f32[1,512]{1,0:T(1,128)} %bitcast.17), custom_call_target="tpu_custom_call" | custom-call | tf_op jit(solution)/shard_map/block_backward/pallas_call | solution.py:628
  42.0 1.8 %hand_over.1 = (bf16[1024,512]{1,0:T(8,128)(2,1)}, f32[9,32,512]{2,1,0:T(8,128)}, f32[1,512]{1,0:T(1,128)}, f32[1,512]{1,0:T(1,128)}) custom-call(bf16[1024,512]{1,0:T(8,128)(2,1)S(1)} %get-tuple-element.11.gin, f32[9,32,512]{2,1,0:T(8,128)S(1)} %get-tuple-element.12.fg, f32[8,128]{1,0:T(8,128)S(1)} %get-tuple-element.13.sums), custom_call_target="tpu_custom_call" | custom-call | tf_op jit(solution)/shard_map/hand_over/pallas_call | solution.py:681

commit v5 on v4

--- a/solution.py
+++ b/solution.py
@@ -53,9 +53,9 @@
 def kernel(
     n, height, width, channels,
     feat_hbm, gout_hbm, filt_hbm, gain_hbm, bias_hbm,
-    gin_ref, fg_ref, sums_ref,
+    gin_ref, fg_ref, gain_row, bias_row,
     feat, featc, gext, filt, gt, act, gact, part, sa, ra, sb, rb, sm, rm, sc, rc, hs, hr, both,
-    gin_s, gin_r, stat, tops, sums, gain_ref, bias_ref,
+    gin_s, gin_r, stat, tops, sums, sums_ref, gain_ref, bias_ref,
     feat_sem, local_sem, push_send, push_recv, halo_send, halo_recv,
     share_send, share_recv,
     out_send, a_recv, b_recv, m_recv, c_recv,
@@ -477,6 +477,9 @@
                 sums_ref[chunks + c * mine + k:chunks + c * mine + k + 1, :] = (
                     everyone[c, mine + k:mine + k + 1]
                 )
+                cols = lanes_of(c * mine + k)
+                bias_row[:, cols] = everyone[c, k:k + 1]
+                gain_row[:, cols] = everyone[c, mine + k:mine + k + 1]
         half_finish(1)
         push_gin.start()
 
@@ -598,18 +601,15 @@
         pass_below.wait_send()
 
 
-def hand_over(gin, fg, sums, gin_out, fg_out, gain_out, bias_out, sem):
-    copies = (
-        pltpu.make_async_copy(gin, gin_out, sem.at[0]),
-        pltpu.make_async_copy(fg, fg_out, sem.at[1]),
-    )
+def hand_over(gin, fg, gain, bias, gin_out, fg_out, gain_out, bias_out, sem):
+    copies = [
+        pltpu.make_async_copy(source, target, sem.at[j])
+        for j, (source, target) in enumerate(
+            ((gin, gin_out), (fg, fg_out), (gain, gain_out), (bias, bias_out))
+        )
+    ]
     for copy in copies:
         copy.start()
-    chunks = sums.shape[0] // 2
-    for c in range(chunks):
-        cols = slice(c * LANES, (c + 1) * LANES)
-        bias_out[:, cols] = sums[c:c + 1, :]
-        gain_out[:, cols] = sums[chunks + c:chunks + c + 1, :]
     for copy in copies:
         copy.wait()
 
@@ -625,15 +625,16 @@
     hbm, vmem = pl.BlockSpec(memory_space=pltpu.HBM), pl.BlockSpec(memory_space=pltpu.VMEM)
     lots = dma((TAPS, mine))
     bits, middle = chips.bit_length() - 1, max(1, chips // 4 - 2)
-    grad_in, filter_grad, sums = pl.pallas_call(
+    results = pl.pallas_call(
         functools.partial(kernel, n, height, width, channels),
         out_shape=(
             jax.ShapeDtypeStruct((slab, channels), BF16),
             jax.ShapeDtypeStruct((TAPS, block, channels), F32),
-            jax.ShapeDtypeStruct((2 * chunks, LANES), F32),
+            jax.ShapeDtypeStruct((1, channels), F32),
+            jax.ShapeDtypeStruct((1, channels), F32),
         ),
         in_specs=[hbm] * 5,
-        out_specs=(vmem, vmem, vmem),
+        out_specs=(vmem,) * 4,
         scratch_shapes=[
             pltpu.VMEM((slab, channels), BF16),
             pltpu.VMEM((area, half), BF16),
@@ -659,6 +660,7 @@
             pltpu.VMEM((n, 1, LANES), F32),
             pltpu.VMEM((n, 1, LANES), F32),
             pltpu.VMEM((n, 2 * mine, LANES), F32),
+            pltpu.VMEM((2 * chunks, LANES), F32),
             pltpu.VMEM((1, channels), F32),
             pltpu.VMEM((1, channels), F32),
             dma((height,)), dma((5,)), dma((3,)), dma((3,)), dma((2,)), dma((2,)),
@@ -686,12 +688,12 @@
             jax.ShapeDtypeStruct((1, channels), F32),
             jax.ShapeDtypeStruct((1, channels), F32),
         ),
-        in_specs=[vmem, vmem, vmem],
-        out_specs=(hbm, hbm, vmem, vmem),
-        scratch_shapes=[dma((2,))],
+        in_specs=[vmem] * 4,
+        out_specs=(hbm,) * 4,
+        scratch_shapes=[dma((4,))],
         compiler_params=pltpu.CompilerParams(vmem_limit_bytes=8 * 1024 * 1024),
         name="hand_over",
-    )(grad_in, filter_grad, sums)
+    )(*results)
     return (
         grad_in.reshape(height, width, channels),
         filter_grad.transpose(1, 0, 2).reshape(block, 3, 3, channels),

time: 43.9 us -> 43.3 us (0.986)
  Pallas kernels: 43.1 us -> 42.5 us
    pallas_call x1, Pallas kernels: 1.76 us -> 1.2 us  [local(): pl.pallas_call(hand_over, out_shape=(jax.ShapeDtypeStruct((slab, channels...]
where the time goes in v5:
time: 43.3 us; the launch traced here: 43.2 us
  Pallas kernels  42.5 us (98%)
  between operations  0.64 us (1%)
    pallas_call x1, Pallas kernels, local(): pl.pallas_call(functools.partial(kernel, n, height, width, channels), out...  41.3 us
    pallas_call x1, Pallas kernels, local(): pl.pallas_call(hand_over, out_shape=(jax.ShapeDtypeStruct((slab, channels...  1.2 us

profile of v5, /device:TPU:0, one launch (start us, length us, event | category | flops | bytes accessed | tf_op | source)
XLA Modules:
  0.0 43.2 jit_solution(13489738452867600906)
XLA Ops:
  0.6 41.3 %block_backward.1 = (bf16[1024,512]{1,0:T(8,128)(2,1)S(1)}, f32[9,32,512]{2,1,0:T(8,128)S(1)}, f32[1,512]{1,0:T(1,128)S(1)}, f32[1,512]{1,0:T(1,128)S(1)}) custom-call(bf16[1024,512]{1,0:T(8,128)(2,1)} %bitcast.14, bf16[1024,512]{1,0:T(8,128)(2,1)} %bitcast.15, bf16[9,512,512]{2,1,0:T(8,128)(2,1)} %bitcast.13, f32[1,512]{1,0:T(1,128)} %bitcast.16, ...), custom_call_target="tpu_custom_call" | custom-call | tf_op jit(solution)/shard_map/block_backward/pallas_call | solution.py:628
  42.0 1.2 %hand_over.1 = (bf16[1024,512]{1,0:T(8,128)(2,1)}, f32[9,32,512]{2,1,0:T(8,128)}, f32[1,512]{1,0:T(1,128)}, f32[1,512]{1,0:T(1,128)}) custom-call(bf16[1024,512]{1,0:T(8,128)(2,1)S(1)} %get-tuple-element.12.gin, f32[9,32,512]{2,1,0:T(8,128)S(1)} %get-tuple-element.13.fg, f32[1,512]{1,0:T(1,128)S(1)} %get-tuple-element.14.gain, ...), custom_call_target="tpu_custom_call" | custom-call | tf_op jit(solution)/shard_map/hand_over/pallas_call | solution.py:683

commit v6 on v5

--- a/solution.py
+++ b/solution.py
@@ -15,7 +15,7 @@
 SWAPPED = 5
 TURNED = 2
 PLAN = (("shift", ), (), ("relay_b", "conv1", "edge_b", ), ("b00", "b01", ), ("b10", "b11", "relay_a", ), ("conv2", "b20", "edge_a", ), ("b30", "conv3", "b40", "c00", ), ("grad", "b50", "c10", "b51", ), ("b21", "b31", "b41", "c01", "c11", "b60", "c20", "c30", ))
-REST = ("b61", "c40", "b70", "c50", "b71", "c51", "c60", "b80", "c61", "d00", "d10", "b81", "c70", "d20", "d30", "c21", "fin1", "c71", "c31", "c41", "fin0", "c80", "c81", "d40", "d50", "d51", "d60", "d61", "d01", "d11", "d70", "d21", "d71", "d31", "d41", "d80", "d81", )
+REST = ("b61", "c40", "b70", "c50", "b71", "c51", "c60", "b80", "c61", "d00", "d10", "b81", "c70", "d20", "d30", "c21", "fin1", "c71", "c31", "c41", "fin0", "c80", "d40", "d50", "d51", "c81", "d60", "d61", "d01", "d11", "d70", "d21", "d71", "d31", "d41", "d80", "d81", )
 MAIN = 40
 EPSILON = 1e-06
 GAIN_MAX = 1.75

time: 43.3 us -> 43.3 us (level)
  no operation moved by 1% of the time
where the time goes in v6:
time: 43.3 us; the launch traced here: 43.2 us
  Pallas kernels  42.5 us (98%)
  between operations  0.64 us (1%)
    pallas_call x1, Pallas kernels, local(): pl.pallas_call(functools.partial(kernel, n, height, width, channels), out...  41.3 us
    pallas_call x1, Pallas kernels, local(): pl.pallas_call(hand_over, out_shape=(jax.ShapeDtypeStruct((slab, channels...  1.2 us

profile of v6, /device:TPU:0, one launch (start us, length us, event | category | flops | bytes accessed | tf_op | source)
XLA Modules:
  0.0 43.2 jit_solution(7979215857774157514)
XLA Ops:
  0.6 41.3 %block_backward.1 = (bf16[1024,512]{1,0:T(8,128)(2,1)S(1)}, f32[9,32,512]{2,1,0:T(8,128)S(1)}, f32[1,512]{1,0:T(1,128)S(1)}, f32[1,512]{1,0:T(1,128)S(1)}) custom-call(bf16[1024,512]{1,0:T(8,128)(2,1)} %bitcast.14, bf16[1024,512]{1,0:T(8,128)(2,1)} %bitcast.15, bf16[9,512,512]{2,1,0:T(8,128)(2,1)} %bitcast.13, f32[1,512]{1,0:T(1,128)} %bitcast.16, ...), custom_call_target="tpu_custom_call" | custom-call | tf_op jit(solution)/shard_map/block_backward/pallas_call | solution.py:628
  42.0 1.2 %hand_over.1 = (bf16[1024,512]{1,0:T(8,128)(2,1)}, f32[9,32,512]{2,1,0:T(8,128)}, f32[1,512]{1,0:T(1,128)}, f32[1,512]{1,0:T(1,128)}) custom-call(bf16[1024,512]{1,0:T(8,128)(2,1)S(1)} %get-tuple-element.12.gin, f32[9,32,512]{2,1,0:T(8,128)S(1)} %get-tuple-element.13.fg, f32[1,512]{1,0:T(1,128)S(1)} %get-tuple-element.14.gain, ...), custom_call_target="tpu_custom_call" | custom-call | tf_op jit(solution)/shard_map/hand_over/pallas_call | solution.py:683
